TPU v7x, 32 devices: a whole 2x2x4 slice. The times are simulated.
32 devices in a mesh: ens: 2 (over y), space: 4 (over z), chan: 2 (over x), sub: 2 (over core).
Axes of the slice: x: 2, y: 2, z: 4, core: 2. Of those that a mesh axis runs over, the one named last changes fastest.
Arguments:
- node_state: bfloat16 [8192, 512], P(('ens', 'space'), ('chan', 'sub')), parts along dimension 0, may hold values from -6 to 6
- norm_gains: float32 [2, 512], replicated, may hold values from 0.25 to 1.75
- norm_shifts: float32 [2, 512], replicated, may hold values from -3 to 3
- query_weight: bfloat16 [512, 512], P(None, 'chan')
- key_weight: bfloat16 [512, 512], P(None, 'chan')
- value_weight: bfloat16 [512, 512], P(None, 'chan'), may hold values from -0.25 to 0.25
- out_weight: bfloat16 [512, 512], replicated, may hold values from -0.25 to 0.25
- ffn_in: bfloat16 [2048, 512], P('chan'), may hold values from -0.25 to 0.25
- ffn_out: bfloat16 [2048, 512], P('chan'), may hold values from -0.125 to 0.125
- live_counts: int32 [4], P('space'), may hold values from 512 to 1024, as said below
- send_rows: int32 [4, 2, 256], P('space'), may hold values from 0 to 1023, as said below
- tile_keys: int32 [32, 12], P('space'), may hold values from 0 to 11, as said below
- tile_bits: int32 [32, 12, 4, 128], P('space'), may hold values from -2147483648 to 2147483647, as said below
Outputs:
- updated: bfloat16 [8192, 512], P(('ens', 'space'), ('chan', 'sub')), parts along dimension 0
There are 2 independent parts, one for each index of `ens`. A program takes and returns all parts, laid end to end along the dimension named above; an argument that names none is the same for every part. Nothing has to cross between parts.
Inputs may be any that keep to these rules, and one draw needn't show every extreme that they name: Partition s has live nodes 0 to live_counts[s] - 1; the first and the last partition are full. send_rows[s, 0] lists nodes of partition s read by its lower neighbour, send_rows[s, 1] those read by its upper neighbour; all are live nodes, and entries may repeat. `tile_keys`: slot 0 of every block names the block itself (its index within the partition); other slots name blocks of the same partition (below 8), of the lower halo (from 8) or of the upper halo (from 10); the first partition names no lower halo and the last no upper halo. `tile_bits`: bit j of word w in column r of a slot says whether query r of the block may attend key 32 w + j of the slot's block (bit 31 is the sign bit); in slot 0 every query's own bit is set. Slots whose words are all zero carry no edges.
All inputs are finite; a program needn't handle non-finite values.
Results may differ from a plain program's by a relative error of at most 0.0095.
Values may be sent and summed in bfloat16 or wider, within the bound.
A program may use at most 64 MiB of HBM per device.

v0:
```python
import math

import jax
import jax.numpy as jnp
from jax import lax
from jax.experimental import pallas as pl
from jax.experimental.pallas import tpu as pltpu
from jax.sharding import PartitionSpec as P

HD = 64


NORM_EPS = 1e-05
NEG_FILL = -1e30


def padded_2(array, sides, width):
    for axis, dim in sides:
        size, length = (lax.axis_size(axis), array.shape[dim])
        up = [(i, (i + 1) % size) for i in range(size - 1)]
        down = [(j, i) for i, j in up]
        last = lax.slice_in_dim(array, length - width, length, axis=dim)
        leading = lax.slice_in_dim(array, 0, width, axis=dim)
        before = lax.ppermute(last, axis, up)
        after = lax.ppermute(leading, axis, down)
        array = jnp.concatenate([before, array, after], axis=dim)
    return array


def normalize_rows(source, gain_row, shift_row):
    row_mean = jnp.mean(source, axis=-1, keepdims=True)
    spread = jnp.mean(source * source, axis=-1, keepdims=True) - row_mean * row_mean
    return (source - row_mean) * lax.rsqrt(spread + NORM_EPS) * gain_row + shift_row


def unpack_allowed(key_bits, key_ids, live_count, tile_size, blocks_own):
    shifts = jnp.arange(32, dtype=jnp.int32)
    expanded = jnp.right_shift(key_bits[..., None, :], shifts[:, None]) & 1
    lead_shape = key_bits.shape[:-2]
    expanded = expanded.reshape(lead_shape + (tile_size, tile_size))
    key_index = key_ids[..., None] * tile_size + jnp.arange(tile_size, dtype=jnp.int32)
    key_live = (key_ids[..., None] >= blocks_own) | (key_index < live_count)
    slot_count = key_ids.shape[-1]
    slot_first = jnp.arange(slot_count, dtype=jnp.int32)[:, None, None] == 0
    diagonal = (
        jnp.arange(tile_size, dtype=jnp.int32)[:, None]
        == jnp.arange(tile_size, dtype=jnp.int32)[None, :]
    )
    own_bit = slot_first & diagonal[None]
    return (expanded == 1) & (key_live[..., None] | own_bit)


def hidden_term(rows, in_piece, out_piece):
    hidden = jax.nn.gelu(
        lax.dot_general(
            rows, in_piece, (((1,), (1,)), ((), ())), preferred_element_type=jnp.float32
        )
    ).astype(jnp.bfloat16)
    return jnp.dot(hidden, out_piece, preferred_element_type=jnp.float32)


def on_device(
    node_state,
    norm_gains,
    norm_shifts,
    query_weight,
    key_weight,
    value_weight,
    out_weight,
    ffn_in,
    ffn_out,
    live_counts,
    send_rows,
    tile_keys,
    tile_bits,
):
    n_chan = lax.axis_size("chan")
    n_sub = lax.axis_size("sub")
    groups = n_chan * n_sub
    chan_at = lax.axis_index("chan")
    sub_at = lax.axis_index("sub")
    node_rank = chan_at * n_sub + sub_at
    node_count = node_state.shape[0]
    tile_size = tile_bits.shape[-1]
    word_count = tile_bits.shape[-2]
    slot_count = tile_keys.shape[1]
    blocks_own = tile_keys.shape[0]
    per_rank = node_count // groups
    head_cols = query_weight.shape[1]
    heads_here = head_cols // HD
    halo_rows = send_rows.shape[-1]
    live_count = live_counts[0]

    def own_half(source):
        step_rows = source.shape[0] // groups
        shaped = source.reshape((n_chan, n_sub, step_rows) + source.shape[1:])
        picked = lax.dynamic_index_in_dim(shaped, sub_at, 1, keepdims=False)
        return picked.reshape((n_chan * step_rows,) + source.shape[1:])

    node_rows = lax.all_to_all(node_state, ("chan", "sub"), split_axis=0, concat_axis=1, tiled=True)
    pair_weight = jnp.concatenate([key_weight, value_weight], axis=1)
    gathered = lax.all_gather(node_state, ("chan", "sub"), axis=1, tiled=True)
    normed = normalize_rows(gathered.astype(jnp.float32), norm_gains[0], norm_shifts[0]).astype(
        jnp.bfloat16
    )
    key_values = jnp.dot(normed, pair_weight, preferred_element_type=jnp.float32).astype(
        jnp.bfloat16
    )
    queries = jnp.dot(own_half(normed), query_weight, preferred_element_type=jnp.float32).astype(
        jnp.bfloat16
    )
    send_list = send_rows.reshape(2 * halo_rows)
    outgoing = jnp.take(key_values, send_list, axis=0)
    padded = padded_2(outgoing, (("space", 0),), halo_rows)
    extended = jnp.concatenate([key_values, padded[:halo_rows], padded[-halo_rows:]], axis=0)
    key_blocks = extended.reshape(-1, tile_size, 2 * head_cols)
    key_ids = own_half(tile_keys)
    key_bits = own_half(tile_bits)
    block_total = key_ids.shape[0]
    per_round = math.gcd(block_total, 4)
    rounds = block_total // per_round
    score_scale = 1.0 / math.sqrt(HD)

    def attend(inputs):
        q_part, id_part, bit_part = inputs
        chosen = key_blocks[id_part]
        keys_part = chosen[..., :head_cols].reshape(
            per_round, slot_count, tile_size, heads_here, HD
        )
        values_part = chosen[..., head_cols:].reshape(
            per_round, slot_count, tile_size, heads_here, HD
        )
        scores = (
            jnp.einsum("grhd,gtkhd->ghrtk", q_part, keys_part, preferred_element_type=jnp.float32)
            * score_scale
        )
        allowed = unpack_allowed(bit_part, id_part, live_count, tile_size, blocks_own)
        allowed = jnp.transpose(allowed, (0, 3, 1, 2))[:, None]
        masked = jnp.where(allowed, scores, NEG_FILL)
        row_max = jnp.max(masked, axis=(3, 4), keepdims=True)
        weights = jnp.where(allowed, jnp.exp(scores - row_max), 0.0)
        row_total = jnp.sum(weights, axis=(3, 4))
        mixed_heads = jnp.einsum(
            "ghrtk,gtkhd->grhd",
            weights.astype(jnp.bfloat16),
            values_part,
            preferred_element_type=jnp.float32,
        )
        mixed_heads = mixed_heads / jnp.transpose(row_total, (0, 2, 1))[..., None]
        return mixed_heads.astype(jnp.bfloat16).reshape(per_round * tile_size, head_cols)

    query_groups = queries.reshape(rounds, per_round, tile_size, heads_here, HD)
    attended = lax.map(
        attend,
        (
            query_groups,
            key_ids.reshape(rounds, per_round, slot_count),
            key_bits.reshape(rounds, per_round, slot_count, word_count, tile_size),
        ),
    )
    mixed_rows = jnp.dot(
        lax.all_to_all(
            attended.reshape(n_chan, per_rank, head_cols),
            "chan",
            split_axis=0,
            concat_axis=2,
            tiled=True,
        )[0],
        out_weight,
        preferred_element_type=jnp.float32,
    )
    after_attn = node_rows.astype(jnp.float32) + mixed_rows
    normed_two = normalize_rows(after_attn, norm_gains[1], norm_shifts[1]).astype(jnp.bfloat16)
    all_rows = lax.all_gather(normed_two, "chan", axis=0, tiled=True)
    update = lax.psum_scatter(
        hidden_term(all_rows, ffn_in, ffn_out).astype(jnp.bfloat16),
        "chan",
        scatter_dimension=0,
        tiled=True,
    ).astype(jnp.float32)
    position = node_rank * per_rank + jnp.arange(per_rank, dtype=jnp.int32)
    result = jnp.where((position < live_count)[:, None], after_attn + update, 0.0).astype(
        jnp.bfloat16
    )
    return lax.all_to_all(result, ("chan", "sub"), split_axis=1, concat_axis=0, tiled=True)


MESH = pl.DeviceIdType.MESH
LOG2E = 1.4426950408889634
NT = (((1,), (1,)), ((), ()))


def gelu_tanh(u):
    inner = 0.7978845608028654 * (u + 0.044715 * (u * u * u))
    return 0.5 * u * (1.0 + jnp.tanh(inner))


def layer_kernel(
    x_hbm,
    gains_hbm,
    shifts_hbm,
    wq_hbm,
    wk_hbm,
    wv_hbm,
    wo_hbm,
    fin_hbm,
    fout_hbm,
    live_ref,
    send_hbm,
    tk_ref,
    bits_hbm,
    out_ref,
    gx,
    hsend,
    nbuf,
    kbuf,
    vbuf,
    wvt,
    qbuf,
    s_ref,
    att,
    own_part,
    psend,
    precv,
    osend,
    wq,
    wk,
    wv,
    wo,
    fin,
    fout,
    gains_ref,
    shifts_ref,
    send_ref,
    bits_ref,
    w_sem,
    loc_sem,
    a_send,
    a_recv,
    b_send,
    b_recv,
    c_send,
    c_recv,
    z_send,
    z_recv,
    t_send,
    t_recv,
    p_send,
    p_recv,
    o_send,
    o_recv,
):
    f32, bf16 = jnp.float32, jnp.bfloat16
    rows, cols = x_hbm.shape
    groups, ext_rows, _ = gx.shape
    tile = bits_hbm.shape[-1]
    words = bits_hbm.shape[-2]
    slots = tk_ref.shape[1]
    blocks_own = tk_ref.shape[0]
    halo = send_hbm.shape[-1]
    head_cols = wq.shape[1]
    pairs = head_cols // (2 * HD)
    pw = 2 * HD
    half_rows = rows // 2
    blocks_here = blocks_own // 2
    chunk = 2 * tile
    n_own = rows // chunk
    per = chunk // tile

    c = lax.axis_index("chan")
    s = lax.axis_index("sub")
    z = lax.axis_index("space")
    nz = lax.axis_size("space")
    own = c * 2 + s
    xslot = (1 - c) * 2 + s
    xdev = {"chan": 1 - c}
    sdev = {"sub": 1 - s}
    has_up = z < nz - 1
    has_down = z > 0

    local = pltpu.make_async_copy(x_hbm, gx.at[own, pl.ds(0, rows)], loc_sem)
    local.start()
    loads = (
        (send_hbm, send_ref),
        (wv_hbm, wv),
        (gains_hbm, gains_ref),
        (shifts_hbm, shifts_ref),
        (wk_hbm, wk),
        (wq_hbm, wq),
        (bits_hbm, bits_ref),
        (wo_hbm, wo),
        (fin_hbm, fin),
        (fout_hbm, fout),
    )
    w_copies = [pltpu.make_async_copy(a, b, w_sem.at[i]) for i, (a, b) in enumerate(loads)]

    barrier = pltpu.get_barrier_semaphore()
    pl.semaphore_signal(barrier, inc=1, device_id=xdev, device_id_type=MESH)
    pl.semaphore_signal(barrier, inc=1, device_id=sdev, device_id_type=MESH)

    @pl.when(has_up)
    def _():
        pl.semaphore_signal(barrier, inc=1, device_id={"space": z + 1}, device_id_type=MESH)

    @pl.when(has_down)
    def _():
        pl.semaphore_signal(barrier, inc=1, device_id={"space": z - 1}, device_id_type=MESH)

    for w_copy in w_copies:
        w_copy.start()
    pl.semaphore_wait(barrier, 2 + jnp.where(has_up, 1, 0) + jnp.where(has_down, 1, 0))

    def rdma(src, dst, ss, rs, dev):
        return pltpu.make_async_remote_copy(
            src_ref=src, dst_ref=dst, send_sem=ss, recv_sem=rs, device_id=dev, device_id_type=MESH
        )

    def a_copy():
        return rdma(gx.at[own, pl.ds(0, rows)], gx.at[own, pl.ds(0, rows)], a_send.at[0], a_recv.at[0], sdev)

    def b_copy(i):
        at = pl.ds(i * chunk, chunk)
        return rdma(gx.at[own, at], gx.at[own, at], b_send.at[i], b_recv.at[i], xdev)

    def c_copy(i):
        at = pl.ds(i * chunk, chunk)
        return rdma(gx.at[xslot, at], gx.at[xslot, at], c_send.at[i], c_recv.at[i], sdev)

    def a2_copy(side):
        part = gx.at[own, pl.ds(rows + side * halo, halo)]
        return rdma(part, part, a_send.at[1 + side], a_recv.at[1 + side], sdev)

    def b2_copy(side):
        part = gx.at[own, pl.ds(rows + side * halo, halo)]
        return rdma(part, part, b_send.at[n_own + side], b_recv.at[n_own + side], xdev)

    def c2_copy(side):
        part = gx.at[xslot, pl.ds(rows + side * halo, halo)]
        return rdma(part, part, c_send.at[n_own + side], c_recv.at[n_own + side], sdev)

    def up_copy():
        return rdma(
            hsend.at[1], gx.at[own, pl.ds(rows, halo)], z_send.at[1], z_recv.at[1], {"space": z + 1}
        )

    def down_copy():
        return rdma(
            hsend.at[0],
            gx.at[own, pl.ds(rows + halo, halo)],
            z_send.at[0],
            z_recv.at[0],
            {"space": z - 1},
        )

    local.wait()
    for i in range(n_own):
        b_copy(i).start()
    a_copy().start()
    w_copies[0].wait()

    lanes = lax.broadcasted_iota(jnp.int32, (halo, tile), 1)
    for side in range(2):
        wanted = jnp.broadcast_to(send_ref[0, side : side + 1, :], (tile, halo)).T
        picks = jnp.concatenate(
            [(wanted == lanes + k * tile).astype(f32).astype(bf16) for k in range(rows // tile)],
            axis=1,
        )
        hsend[side] = jnp.dot(picks, gx[own, pl.ds(0, rows)], preferred_element_type=f32).astype(bf16)

    @pl.when(has_up)
    def _():
        up_copy().start()

    @pl.when(has_down)
    def _():
        down_copy().start()

    @pl.when(jnp.logical_not(has_down))
    def _():
        gx[own, pl.ds(rows, halo)] = jnp.zeros((halo, cols), bf16)

    @pl.when(jnp.logical_not(has_up))
    def _():
        gx[own, pl.ds(rows + halo, halo)] = jnp.zeros((halo, cols), bf16)

    for i in range(1, 5):
        w_copies[i].wait()
    wvt[...] = wv[...].astype(f32).T.astype(bf16)
    a_copy().wait_recv()

    def full_rows(at):
        return jnp.concatenate([gx[g, at] for g in range(groups)], axis=1).astype(f32)

    def norm(v, which):
        mean = jnp.mean(v, axis=-1, keepdims=True)
        spread = jnp.mean(v * v, axis=-1, keepdims=True) - mean * mean
        scaled = (v - mean) * lax.rsqrt(spread + NORM_EPS)
        return scaled * gains_ref[which : which + 1, :] + shifts_ref[which : which + 1, :]

    def project(i, keep):
        at = pl.ds(pl.multiple_of(i * chunk, chunk), chunk)
        normed = norm(full_rows(at), 0).astype(bf16)
        if keep:
            nbuf[at] = normed
        keys = jnp.dot(normed, wk[...], preferred_element_type=f32).astype(bf16)
        values = lax.dot_general(wvt[...], normed, NT, preferred_element_type=f32).astype(bf16)
        for k in range(per):
            kbuf[i * per + k] = keys[k * tile : (k + 1) * tile]
            vbuf[i * per + k] = values[:, k * tile : (k + 1) * tile]

    b_copy(0).wait_recv()
    c_copy(0).start()

    def own_step(i, carry):
        b_copy(i).wait_recv()
        c_copy(i).start()
        c_copy(i - 1).wait_recv()
        project(i - 1, True)
        return carry

    lax.fori_loop(1, n_own - 1, own_step, 0)

    @pl.when(has_down)
    def _():
        up_copy().wait_recv()

    b2_copy(0).start()
    a2_copy(0).start()

    @pl.when(has_up)
    def _():
        down_copy().wait_recv()

    b2_copy(1).start()
    a2_copy(1).start()
    lax.fori_loop(n_own - 1, n_own, own_step, 0)
    c_copy(n_own - 1).wait_recv()
    project(n_own - 1, True)

    scale = LOG2E / math.sqrt(HD)
    w_copies[5].wait()
    own_at = pl.ds(pl.multiple_of(s * half_rows, half_rows), half_rows)
    q_rows = jnp.dot(nbuf[own_at], wq[...], preferred_element_type=f32) * scale
    qbuf[...] = q_rows.astype(bf16)
    w_copies[6].wait()
    per_side = halo // chunk

    def halo_step(i, carry):
        project(i, False)
        return carry

    b2_copy(0).wait_recv()
    c2_copy(0).start()
    a2_copy(0).wait_recv()
    c2_copy(0).wait_recv()
    lax.fori_loop(n_own, n_own + per_side, halo_step, 0)
    b2_copy(1).wait_recv()
    c2_copy(1).start()
    a2_copy(1).wait_recv()
    c2_copy(1).wait_recv()
    lax.fori_loop(n_own + per_side, n_own + 2 * per_side, halo_step, 0)

    live = live_ref[0]
    word_rows = tile // words
    row_id = lax.broadcasted_iota(jnp.int32, (tile, tile), 0)
    col_id = lax.broadcasted_iota(jnp.int32, (tile, tile), 1)
    shifts = lax.broadcasted_iota(jnp.int32, (word_rows, tile), 0)
    low_half = lax.broadcasted_iota(jnp.int32, (tile, pw), 1) < HD

    def t_copy(j):
        at = pl.ds(j * tile, tile)
        return rdma(att.at[c, at], att.at[c, at], t_send.at[j], t_recv.at[j], xdev)

    ones = jnp.ones((16, 2 * tile), bf16)

    def attend_block(j, carry):
        b = s * blocks_here + j
        ids = [tk_ref[b, t] for t in range(slots)]
        q_rows = qbuf[pl.ds(pl.multiple_of(j * tile, tile), tile)]
        wide = []
        for pair in range(pairs):
            q_pair = q_rows[:, pair * pw : (pair + 1) * pw]
            zero = jnp.zeros_like(q_pair)
            wide.append(
                jnp.concatenate(
                    [jnp.where(low_half, q_pair, zero), jnp.where(low_half, zero, q_pair)], axis=0
                )
            )
        tops = [jnp.full((8, 2 * tile), NEG_FILL, f32) for _ in range(pairs)]
        for t in range(slots):
            block_bits = bits_ref[b, t]
            set_bits = jnp.concatenate(
                [
                    jnp.right_shift(
                        jnp.broadcast_to(block_bits[w : w + 1, :], (word_rows, tile)), shifts
                    )
                    & 1
                    for w in range(words)
                ],
                axis=0,
            )
            limit = jnp.where(ids[t] >= blocks_own, tile, live - ids[t] * tile)
            good = row_id < limit
            if t == 0:
                good = good | (row_id == col_id)
            bias = jnp.where((set_bits == 1) & good, 0.0, NEG_FILL)
            bias = jnp.concatenate([bias, bias], axis=1)
            for pair in range(pairs):
                keys = kbuf[ids[t], :, pair * pw : (pair + 1) * pw]
                scores = lax.dot_general(keys, wide[pair], NT, preferred_element_type=f32) + bias
                s_ref[pair, t * tile : (t + 1) * tile] = scores
                tops[pair] = jnp.maximum(
                    tops[pair], jnp.max(scores.reshape(tile // 8, 8, 2 * tile), axis=0)
                )
        pieces = []
        for pair in range(pairs):
            top = jnp.max(tops[pair], axis=0, keepdims=True)
            mixed = jnp.zeros((pw + 16, 2 * tile), f32)
            for t in range(0, slots, 2):
                p = jnp.exp2(s_ref[pair, t * tile : (t + 2) * tile] - top).astype(bf16)
                at = slice(pair * pw, (pair + 1) * pw)
                values = jnp.concatenate([vbuf[ids[t], at], vbuf[ids[t + 1], at]], axis=1)
                values = jnp.concatenate([values, ones], axis=0)
                mixed = mixed + jnp.dot(values, p, preferred_element_type=f32)
            inverse = 1.0 / mixed[pw : pw + 1]
            pieces.append(mixed[:HD, :tile] * inverse[:, :tile])
            pieces.append(mixed[HD:pw, tile:] * inverse[:, tile:])
        att[c, pl.ds(pl.multiple_of(j * tile, tile), tile)] = (
            jnp.concatenate(pieces, axis=0).T.astype(bf16)
        )
        t_copy(j).start()
        return carry

    lax.fori_loop(0, blocks_here, attend_block, 0)

    for i in (7, 8, 9):
        w_copies[i].wait()

    n_ffn = half_rows // chunk

    def p_copy(i):
        at = pl.ds(i * chunk, chunk)
        return rdma(psend.at[at], precv.at[at], p_send.at[i], p_recv.at[i], xdev)

    def ffn_chunk(i, carry):
        for k in range(per):
            t_copy(i * per + k).wait_recv()
        at = pl.ds(pl.multiple_of(i * chunk, chunk), chunk)
        rows_at = pl.ds(pl.multiple_of(s * half_rows + i * chunk, chunk), chunk)
        mixed = jnp.concatenate([att[g, at] for g in range(groups // 2)], axis=1)
        after = full_rows(rows_at) + jnp.dot(mixed, wo[...], preferred_element_type=f32)
        normed_two = norm(after, 1).astype(bf16)
        hidden = gelu_tanh(
            lax.dot_general(normed_two, fin[...], NT, preferred_element_type=f32)
        ).astype(bf16)
        part = jnp.dot(hidden, fout[...], preferred_element_type=f32)
        left, right = part[:, :head_cols], part[:, head_cols:]
        first = c == 0
        psend[at] = jnp.where(first, right, left).astype(bf16)
        p_copy(i).start()
        own_part[at] = jnp.where(first, left + after[:, :head_cols], right + after[:, head_cols:])
        return carry

    lax.fori_loop(0, n_ffn, ffn_chunk, 0)

    def o_copy(i):
        at = pl.ds(i * chunk, chunk)
        out_at = pl.ds(s * half_rows + i * chunk, chunk)
        return rdma(osend.at[at], out_ref.at[out_at], o_send.at[i], o_recv.at[i], sdev)

    def finish(i, carry):
        p_copy(i).wait_recv()
        at = pl.ds(pl.multiple_of(i * chunk, chunk), chunk)
        base = s * half_rows + i * chunk
        summed = own_part[at] + precv[at].astype(f32)
        position = base + lax.broadcasted_iota(jnp.int32, (chunk, head_cols), 0)
        done = jnp.where(position < live, summed, 0.0)
        left, right = done[:, :cols], done[:, cols:]
        first = s == 0
        osend[at] = jnp.where(first, right, left).astype(bf16)
        o_copy(i).start()
        out_ref[pl.ds(pl.multiple_of(base, chunk), chunk)] = jnp.where(
            first, left, right
        ).astype(bf16)
        return carry

    lax.fori_loop(0, n_ffn, finish, 0)

    a_copy().wait_send()
    for side in range(2):
        a2_copy(side).wait_send()
        b2_copy(side).wait_send()
        c2_copy(side).wait_send()
    for i in range(n_own):
        b_copy(i).wait_send()
        c_copy(i).wait_send()
    for j in range(blocks_here):
        t_copy(j).wait_send()

    @pl.when(has_up)
    def _():
        up_copy().wait_send()

    @pl.when(has_down)
    def _():
        down_copy().wait_send()

    for i in range(n_ffn):
        p_copy(i).wait_send()
        o_copy(i).wait()


def one_kernel(*args):
    (x, gains, shifts, wq, wk, wv, wo, fin, fout, live, send, tk, bits) = args
    bf16 = jnp.bfloat16
    rows, cols = x.shape
    width = gains.shape[1]
    groups = lax.axis_size("chan") * lax.axis_size("sub")
    halo = send.shape[-1]
    tile = bits.shape[-1]
    slots = tk.shape[1]
    ext = rows + 2 * halo
    head_cols = wq.shape[1]
    half = rows // 2
    chunk = 2 * tile
    n_own = rows // chunk
    blocks_here = tk.shape[0] // 2
    n_ffn = half // chunk
    vmem = pltpu.VMEM
    dma = pltpu.SemaphoreType.DMA
    in_vmem = pl.BlockSpec(memory_space=pltpu.VMEM)
    in_smem = pl.BlockSpec(memory_space=pltpu.SMEM)
    in_any = pl.BlockSpec(memory_space=pl.ANY)
    return pl.pallas_call(
        layer_kernel,
        out_shape=pltpu.VMEM(x.shape, bf16),
        in_specs=[in_any] * 9 + [in_smem, in_any, in_smem, in_any],
        out_specs=in_vmem,
        scratch_shapes=[
            vmem((groups, ext, cols), bf16),
            vmem((2, halo, cols), bf16),
            vmem((rows, width), bf16),
            vmem((ext // tile, tile, head_cols), bf16),
            vmem((ext // tile, head_cols, tile), bf16),
            vmem((head_cols, width), bf16),
            vmem((half, head_cols), bf16),
            vmem((head_cols // (2 * HD), slots * tile, 2 * tile), jnp.float32),
            vmem((2, half, head_cols), bf16),
            vmem((half, head_cols), jnp.float32),
            vmem((half, head_cols), bf16),
            vmem((half, head_cols), bf16),
            vmem((half, cols), bf16),
            vmem(wq.shape, bf16),
            vmem(wk.shape, bf16),
            vmem(wv.shape, bf16),
            vmem(wo.shape, bf16),
            vmem(fin.shape, bf16),
            vmem(fout.shape, bf16),
            vmem(gains.shape, jnp.float32),
            vmem(shifts.shape, jnp.float32),
            vmem(send.shape, jnp.int32),
            vmem(bits.shape, jnp.int32),
            dma((10,)),
            dma,
            dma((3,)),
            dma((3,)),
            dma((n_own + 2,)),
            dma((n_own + 2,)),
            dma((n_own + 2,)),
            dma((n_own + 2,)),
            dma((2,)),
            dma((2,)),
            dma((blocks_here,)),
            dma((blocks_here,)),
            dma((n_ffn,)),
            dma((n_ffn,)),
            dma((n_ffn,)),
            dma((n_ffn,)),
        ],
        compiler_params=pltpu.CompilerParams(collective_id=0, has_side_effects=True),
    )(*args)


def on_any_device(*args):
    two_by_two = lax.axis_size("chan") == 2 and lax.axis_size("sub") == 2
    cols, head_cols = args[0].shape[1], args[3].shape[1]
    tile, halo = args[12].shape[-1], args[10].shape[-1]
    rows_fit = args[0].shape[0] % (4 * tile) == 0 and halo % (2 * tile) == 0
    if two_by_two and cols % 128 == 0 and head_cols % (2 * HD) == 0 and rows_fit and args[11].shape[1] % 2 == 0:
        return one_kernel(*args)
    return on_device(*args)


def solution(mesh):
    in_specs = (
        P(("ens", "space"), ("chan", "sub")),
        P(),
        P(),
        P(None, "chan"),
        P(None, "chan"),
        P(None, "chan"),
        P(),
        P("chan", None),
        P("chan", None),
        P("space"),
        P("space", None, None),
        P("space", None),
        P("space", None, None, None),
    )
    out_specs = P(("ens", "space"), ("chan", "sub"))
    return jax.shard_map(
        on_any_device, mesh=mesh, in_specs=in_specs, out_specs=out_specs, check_vma=False
    )
```

profile of v0, /device:TPU:0, one launch (start us, length us, event | category | flops | bytes accessed | tf_op | source)
XLA Modules:
  0.0 35.4 jit_solution(13027990752875815899)
XLA Ops:
  0.7 34.0 %shard_map.127 = bf16[1024,128]{1,0:T(8,128)(2,1)S(1)} custom-call(bf16[1024,128]{1,0:T(8,128)(2,1)} %x_hbm.1, f32[2,512]{1,0:T(2,128)} %gains_hbm.1, f32[2,512]{1,0:T(2,128)} %shifts_hbm.1, bf16[512,256]{1,0:T(8,128)(2,1)} %wq_hbm.1, bf16[512,256]{1,0:T(8,128)(2,1)} %wk_hbm.1, bf16[512,256]{1,0:T(8,128)(2,1)} %wv_hbm.1, bf16[512,512]{1,0:T(8,128)(2,1)} %wo_hbm.1, ...), custom_call_target="tpu_custom_call" | custom-call | tf_op jit(solution)/shard_map/pallas_call | solution.py:634
  34.6 0.7 %copy.15 = bf16[1024,128]{1,0:T(8,128)(2,1)} copy(bf16[1024,128]{1,0:T(8,128)(2,1)S(1)} %shard_map.127) | data formatting | bytes 524288
where the time goes:
time: 35.5 us; the launch traced here: 35.4 us
  Pallas kernels  34 us (96%)
  local copies, waits for them, and re-layouts  0.71 us (2%)
  between operations  0.66 us (2%)
    pallas_call x1, Pallas kernels, one_kernel(): pl.pallas_call(layer_kernel, out_shape=pltpu.VMEM(x.shape, bf16), in_spec...  34 us

commit v1 on v0

v1 whole, which is shorter than its diff:
```python
import math

import jax
import jax.numpy as jnp
from jax import lax
from jax.experimental import pallas as pl
from jax.experimental.pallas import tpu as pltpu
from jax.sharding import PartitionSpec as P

HD = 64


NORM_EPS = 1e-05
NEG_FILL = -1e30


def padded_2(array, sides, width):
    for axis, dim in sides:
        size, length = (lax.axis_size(axis), array.shape[dim])
        up = [(i, (i + 1) % size) for i in range(size - 1)]
        down = [(j, i) for i, j in up]
        last = lax.slice_in_dim(array, length - width, length, axis=dim)
        leading = lax.slice_in_dim(array, 0, width, axis=dim)
        before = lax.ppermute(last, axis, up)
        after = lax.ppermute(leading, axis, down)
        array = jnp.concatenate([before, array, after], axis=dim)
    return array


def normalize_rows(source, gain_row, shift_row):
    row_mean = jnp.mean(source, axis=-1, keepdims=True)
    spread = jnp.mean(source * source, axis=-1, keepdims=True) - row_mean * row_mean
    return (source - row_mean) * lax.rsqrt(spread + NORM_EPS) * gain_row + shift_row


def unpack_allowed(key_bits, key_ids, live_count, tile_size, blocks_own):
    shifts = jnp.arange(32, dtype=jnp.int32)
    expanded = jnp.right_shift(key_bits[..., None, :], shifts[:, None]) & 1
    lead_shape = key_bits.shape[:-2]
    expanded = expanded.reshape(lead_shape + (tile_size, tile_size))
    key_index = key_ids[..., None] * tile_size + jnp.arange(tile_size, dtype=jnp.int32)
    key_live = (key_ids[..., None] >= blocks_own) | (key_index < live_count)
    slot_count = key_ids.shape[-1]
    slot_first = jnp.arange(slot_count, dtype=jnp.int32)[:, None, None] == 0
    diagonal = (
        jnp.arange(tile_size, dtype=jnp.int32)[:, None]
        == jnp.arange(tile_size, dtype=jnp.int32)[None, :]
    )
    own_bit = slot_first & diagonal[None]
    return (expanded == 1) & (key_live[..., None] | own_bit)


def hidden_term(rows, in_piece, out_piece):
    hidden = jax.nn.gelu(
        lax.dot_general(
            rows, in_piece, (((1,), (1,)), ((), ())), preferred_element_type=jnp.float32
        )
    ).astype(jnp.bfloat16)
    return jnp.dot(hidden, out_piece, preferred_element_type=jnp.float32)


def on_device(
    node_state,
    norm_gains,
    norm_shifts,
    query_weight,
    key_weight,
    value_weight,
    out_weight,
    ffn_in,
    ffn_out,
    live_counts,
    send_rows,
    tile_keys,
    tile_bits,
):
    n_chan = lax.axis_size("chan")
    n_sub = lax.axis_size("sub")
    groups = n_chan * n_sub
    chan_at = lax.axis_index("chan")
    sub_at = lax.axis_index("sub")
    node_rank = chan_at * n_sub + sub_at
    node_count = node_state.shape[0]
    tile_size = tile_bits.shape[-1]
    word_count = tile_bits.shape[-2]
    slot_count = tile_keys.shape[1]
    blocks_own = tile_keys.shape[0]
    per_rank = node_count // groups
    head_cols = query_weight.shape[1]
    heads_here = head_cols // HD
    halo_rows = send_rows.shape[-1]
    live_count = live_counts[0]

    def own_half(source):
        step_rows = source.shape[0] // groups
        shaped = source.reshape((n_chan, n_sub, step_rows) + source.shape[1:])
        picked = lax.dynamic_index_in_dim(shaped, sub_at, 1, keepdims=False)
        return picked.reshape((n_chan * step_rows,) + source.shape[1:])

    node_rows = lax.all_to_all(node_state, ("chan", "sub"), split_axis=0, concat_axis=1, tiled=True)
    pair_weight = jnp.concatenate([key_weight, value_weight], axis=1)
    gathered = lax.all_gather(node_state, ("chan", "sub"), axis=1, tiled=True)
    normed = normalize_rows(gathered.astype(jnp.float32), norm_gains[0], norm_shifts[0]).astype(
        jnp.bfloat16
    )
    key_values = jnp.dot(normed, pair_weight, preferred_element_type=jnp.float32).astype(
        jnp.bfloat16
    )
    queries = jnp.dot(own_half(normed), query_weight, preferred_element_type=jnp.float32).astype(
        jnp.bfloat16
    )
    send_list = send_rows.reshape(2 * halo_rows)
    outgoing = jnp.take(key_values, send_list, axis=0)
    padded = padded_2(outgoing, (("space", 0),), halo_rows)
    extended = jnp.concatenate([key_values, padded[:halo_rows], padded[-halo_rows:]], axis=0)
    key_blocks = extended.reshape(-1, tile_size, 2 * head_cols)
    key_ids = own_half(tile_keys)
    key_bits = own_half(tile_bits)
    block_total = key_ids.shape[0]
    per_round = math.gcd(block_total, 4)
    rounds = block_total // per_round
    score_scale = 1.0 / math.sqrt(HD)

    def attend(inputs):
        q_part, id_part, bit_part = inputs
        chosen = key_blocks[id_part]
        keys_part = chosen[..., :head_cols].reshape(
            per_round, slot_count, tile_size, heads_here, HD
        )
        values_part = chosen[..., head_cols:].reshape(
            per_round, slot_count, tile_size, heads_here, HD
        )
        scores = (
            jnp.einsum("grhd,gtkhd->ghrtk", q_part, keys_part, preferred_element_type=jnp.float32)
            * score_scale
        )
        allowed = unpack_allowed(bit_part, id_part, live_count, tile_size, blocks_own)
        allowed = jnp.transpose(allowed, (0, 3, 1, 2))[:, None]
        masked = jnp.where(allowed, scores, NEG_FILL)
        row_max = jnp.max(masked, axis=(3, 4), keepdims=True)
        weights = jnp.where(allowed, jnp.exp(scores - row_max), 0.0)
        row_total = jnp.sum(weights, axis=(3, 4))
        mixed_heads = jnp.einsum(
            "ghrtk,gtkhd->grhd",
            weights.astype(jnp.bfloat16),
            values_part,
            preferred_element_type=jnp.float32,
        )
        mixed_heads = mixed_heads / jnp.transpose(row_total, (0, 2, 1))[..., None]
        return mixed_heads.astype(jnp.bfloat16).reshape(per_round * tile_size, head_cols)

    query_groups = queries.reshape(rounds, per_round, tile_size, heads_here, HD)
    attended = lax.map(
        attend,
        (
            query_groups,
            key_ids.reshape(rounds, per_round, slot_count),
            key_bits.reshape(rounds, per_round, slot_count, word_count, tile_size),
        ),
    )
    mixed_rows = jnp.dot(
        lax.all_to_all(
            attended.reshape(n_chan, per_rank, head_cols),
            "chan",
            split_axis=0,
            concat_axis=2,
            tiled=True,
        )[0],
        out_weight,
        preferred_element_type=jnp.float32,
    )
    after_attn = node_rows.astype(jnp.float32) + mixed_rows
    normed_two = normalize_rows(after_attn, norm_gains[1], norm_shifts[1]).astype(jnp.bfloat16)
    all_rows = lax.all_gather(normed_two, "chan", axis=0, tiled=True)
    update = lax.psum_scatter(
        hidden_term(all_rows, ffn_in, ffn_out).astype(jnp.bfloat16),
        "chan",
        scatter_dimension=0,
        tiled=True,
    ).astype(jnp.float32)
    position = node_rank * per_rank + jnp.arange(per_rank, dtype=jnp.int32)
    result = jnp.where((position < live_count)[:, None], after_attn + update, 0.0).astype(
        jnp.bfloat16
    )
    return lax.all_to_all(result, ("chan", "sub"), split_axis=1, concat_axis=0, tiled=True)


MESH = pl.DeviceIdType.MESH
LOG2E = 1.4426950408889634
NT = (((1,), (1,)), ((), ()))


def gelu_tanh(u):
    inner = 0.7978845608028654 * (u + 0.044715 * (u * u * u))
    return 0.5 * u * (1.0 + jnp.tanh(inner))


def layer_kernel(
    x_hbm,
    gains_hbm,
    shifts_hbm,
    wq_hbm,
    wk_hbm,
    wv_hbm,
    wo_hbm,
    fin_hbm,
    fout_hbm,
    live_hbm,
    send_hbm,
    tk_hbm,
    bits_hbm,
    out_ref,
    xq,
    gx,
    hsend,
    kv,
    wvt,
    qbuf,
    bias_ref,
    s_ref,
    att,
    full_part,
    half_part,
    from_sib,
    from_x,
    proj_w,
    ffn_w,
    norm_ref,
    send_ref,
    bits_ref,
    live_ref,
    tk_ref,
    w_sem,
    loc_sem,
    a_send,
    a_recv,
    x_send,
    x_recv,
    z_send,
    z_recv,
    h_send,
    h_recv,
    k_send,
    k_recv,
    t_send,
    t_recv,
    p_send,
    p_recv,
    d_send,
    d_recv,
):
    f32, bf16 = jnp.float32, jnp.bfloat16
    rows, cols = x_hbm.shape
    groups = gx.shape[0]
    tile = bits_hbm.shape[-1]
    words = bits_hbm.shape[-2]
    slots = tk_ref.shape[1]
    blocks_own = tk_ref.shape[0]
    halo = send_hbm.shape[-1]
    width, head_cols = wv_hbm.shape
    hidden_here = fin_hbm.shape[0]
    pw = 2 * HD
    pairs = head_cols // pw
    half = rows // 2
    n_here = half // tile
    n_halo = halo // tile

    c = lax.axis_index("chan")
    s = lax.axis_index("sub")
    z = lax.axis_index("space")
    nz = lax.axis_size("space")
    own = c * 2 + s
    sib = c * 2 + 1 - s
    far = (1 - c) * 2
    xdev = {"chan": 1 - c}
    sdev = {"sub": 1 - s}
    has_up = z < nz - 1
    has_down = z > 0
    has_halo = jnp.where(s == 0, z, nz - 1 - z) > 0

    own_half = pl.ds(pl.multiple_of(s * half, half), half)
    sib_half = pl.ds(pl.multiple_of((1 - s) * half, half), half)
    local = pltpu.make_async_copy(x_hbm, xq, loc_sem.at[0])
    local_own = pltpu.make_async_copy(x_hbm.at[own_half], gx.at[own, pl.ds(0, half)], loc_sem.at[1])
    fin = ffn_w.at[pl.ds(0, hidden_here)]
    fout = ffn_w.at[pl.ds(hidden_here, hidden_here)]
    wo = ffn_w.at[pl.ds(2 * hidden_here, width)]
    n_norms = gains_hbm.shape[0]
    loads = (
        (send_hbm, send_ref, 0),
        (tk_hbm, tk_ref, 1),
        (live_hbm, live_ref, 2),
        (bits_hbm, bits_ref, 3),
        (wv_hbm, proj_w.at[:, pl.ds(2 * head_cols, head_cols)], 4),
        (gains_hbm, norm_ref.at[pl.ds(0, n_norms)], 5),
        (shifts_hbm, norm_ref.at[pl.ds(n_norms, n_norms)], 5),
        (wk_hbm, proj_w.at[:, pl.ds(0, head_cols)], 4),
        (wq_hbm, proj_w.at[:, pl.ds(head_cols, head_cols)], 4),
        (wo_hbm, wo, 6),
        (fin_hbm, fin, 6),
        (fout_hbm, fout, 6),
    )
    landed = (send_ref, tk_ref, live_ref, bits_ref, proj_w, norm_ref, ffn_w)

    def loaded(i):
        pltpu.make_async_copy(landed[i], landed[i], w_sem.at[i]).wait()


    barrier = pltpu.get_barrier_semaphore()

    def greet(dev):
        pl.semaphore_signal(barrier, inc=1, device_id=dev, device_id_type=MESH)

    greet(xdev)
    greet({"chan": 1 - c, "sub": 1 - s})
    greet(sdev)

    @pl.when(has_up)
    def _():
        greet({"space": z + 1})
        greet({"space": z + 1, "sub": 1 - s})

    @pl.when(has_down)
    def _():
        greet({"space": z - 1})
        greet({"space": z - 1, "sub": 1 - s})

    local.start()
    local_own.start()
    for a, b, i in loads:
        pltpu.make_async_copy(a, b, w_sem.at[i]).start()
    with jax.named_scope("barrierw"):
        pl.semaphore_wait(barrier, 3 + jnp.where(has_up, 2, 0) + jnp.where(has_down, 2, 0))
        local.wait()

    def rdma(src, dst, ss, rs, dev):
        return pltpu.make_async_remote_copy(
            src_ref=src, dst_ref=dst, send_sem=ss, recv_sem=rs, device_id=dev, device_id_type=MESH
        )

    def block(i):
        return pl.ds(pl.multiple_of(i * tile, tile), tile)

    def a_copy():
        return rdma(xq.at[sib_half], gx.at[own, pl.ds(0, half)], a_send, a_recv, sdev)

    def a_wait():
        part = gx.at[sib, pl.ds(0, half)]
        rdma(part, part, a_send, a_recv, sdev).wait_recv()

    def x_copy(i, to):
        src = xq.at[pl.ds(to * half + i * tile, tile)]
        dev = {"chan": 1 - c, "sub": to}
        return rdma(src, gx.at[own, block(i)], x_send, x_recv.at[i], dev)

    def x_wait(i):
        part = gx.at[pl.ds(far, 2), block(i)]
        rdma(part, part, x_send, x_recv.at[i], xdev).wait_recv()

    halo_at = pl.ds(half, halo)

    def z_copy(side):
        if side == 1:
            dev = {"space": z + 1, "sub": 0}
        else:
            dev = {"space": z - 1, "sub": 1}
        return rdma(hsend.at[side], gx.at[own, halo_at], z_send.at[side], z_recv, dev)

    def z_wait():
        part = gx.at[pl.ds(c * 2, 2), halo_at]
        rdma(part, part, z_send.at[0], z_recv, sdev).wait_recv()

    def h_copy(k):
        part = gx.at[pl.ds(c * 2, 2), pl.ds(half + k * tile, tile)]
        return rdma(part, part, h_send, h_recv.at[k], xdev)

    def h_wait(k):
        part = gx.at[pl.ds(far, 2), pl.ds(half + k * tile, tile)]
        rdma(part, part, h_send, h_recv.at[k], xdev).wait_recv()

    for i in range(n_here):
        x_copy(i, 0).start()
        x_copy(i, 1).start()
    a_copy().start()
    loaded(0)

    with jax.named_scope("onehot"):
        lanes = lax.broadcasted_iota(jnp.int32, (halo, tile), 1)
        for side in range(2):
            wanted = jnp.broadcast_to(send_ref[0, side : side + 1, :], (tile, halo)).T
            picks = jnp.concatenate(
                [(wanted == lanes + k * tile).astype(f32).astype(bf16) for k in range(rows // tile)],
                axis=1,
            )
            hsend[side] = jnp.dot(picks, xq[...], preferred_element_type=f32).astype(bf16)

    @pl.when(has_up)
    def _():
        z_copy(1).start()

    @pl.when(has_down)
    def _():
        z_copy(0).start()

    @pl.when(jnp.logical_not(has_halo))
    def _():
        gx[:, halo_at, :] = jnp.zeros((groups, halo, cols), bf16)

    for i in range(1, 5):
        loaded(i)
    wvt[...] = proj_w[:, 2 * head_cols :].astype(f32).T.astype(bf16)

    live = live_ref[0]
    word_rows = tile // words
    row_id = lax.broadcasted_iota(jnp.int32, (tile, tile), 0)
    col_id = lax.broadcasted_iota(jnp.int32, (tile, tile), 1)
    shifts = lax.broadcasted_iota(jnp.int32, (word_rows, tile), 0)
    low_half = lax.broadcasted_iota(jnp.int32, (tile, pw), 1) < HD

    def mask_block(j, carry):
        b = s * n_here + j
        for t in range(slots):
            slot_id = tk_ref[b, t]
            block_bits = bits_ref[b, t]
            set_bits = jnp.concatenate(
                [
                    jnp.right_shift(
                        jnp.broadcast_to(block_bits[w : w + 1, :], (word_rows, tile)), shifts
                    )
                    & 1
                    for w in range(words)
                ],
                axis=0,
            )
            limit = jnp.where(slot_id >= blocks_own, tile, live - slot_id * tile)
            good = row_id < limit
            if t == 0:
                good = good | (row_id == col_id)
            bias_ref[j, t * tile : (t + 1) * tile] = jnp.where(
                (set_bits == 1) & good, 0.0, NEG_FILL
            )
        return carry

    with jax.named_scope("mask"):
        lax.fori_loop(0, n_here, mask_block, 0)

    def full_rows(at):
        return jnp.concatenate([gx[g, at] for g in range(groups)], axis=1).astype(f32)

    def norm(v, which):
        mean = jnp.mean(v, axis=-1, keepdims=True)
        spread = jnp.mean(v * v, axis=-1, keepdims=True) - mean * mean
        scaled = (v - mean) * lax.rsqrt(spread + NORM_EPS)
        gain, shift = norm_ref[which : which + 1, :], norm_ref[n_norms + which : n_norms + which + 1, :]
        return scaled * gain + shift

    scale = LOG2E / math.sqrt(HD)

    per_core = n_here + n_halo

    def k_copy(core, i):
        part = kv.at[core * per_core + i]
        return rdma(part, part, k_send.at[0], k_recv.at[i], sdev)

    def project(i, with_queries):
        normed = norm(full_rows(block(i)), 0).astype(bf16)
        to = s * per_core + i
        wanted = (2 if with_queries else 1) * head_cols
        both = jnp.dot(normed, proj_w[:, :wanted], preferred_element_type=f32)
        for pair in range(pairs):
            kv[to, pair] = both[:, pair * pw : (pair + 1) * pw].astype(bf16)
        if with_queries:
            qbuf[block(i)] = (both[:, head_cols:] * scale).astype(bf16)
        values = lax.dot_general(wvt[...], normed, NT, preferred_element_type=f32)
        for pair in range(pairs):
            kv[to, pairs + pair] = values[pair * pw : (pair + 1) * pw].astype(bf16)
        k_copy(s, i).start()

    loaded(5)
    local_own.wait()
    with jax.named_scope("aw"):
        a_wait()

    def own_step(i, carry):
        with jax.named_scope("xw"):
            x_wait(i)
        with jax.named_scope("proj"):
            project(i, True)
        return carry

    early = n_here // 2
    lax.fori_loop(0, early, own_step, 0)

    with jax.named_scope("zw"):

        @pl.when(has_halo)
        def _():
            z_wait()
            for k in range(n_halo):
                h_copy(k).start()

    lax.fori_loop(early, n_here, own_step, 0)
    for k in range(n_halo):
        with jax.named_scope("hw"):

            @pl.when(has_halo)
            def _():
                h_wait(k)

        with jax.named_scope("hproj"):
            project(n_here + k, False)

    with jax.named_scope("kvw"):
        for i in range(n_here + n_halo):
            k_copy(1 - s, i).wait_recv()

    def t_copy(j):
        part = att.at[pl.ds(c * pairs, pairs), block(j)]
        return rdma(part, part, t_send, t_recv.at[j], xdev)

    def t_wait(j):
        part = att.at[pl.ds((1 - c) * pairs, pairs), block(j)]
        rdma(part, part, t_send, t_recv.at[j], xdev).wait_recv()

    def stored(block_id):
        halo_id = block_id - blocks_own
        in_own = block_id // n_here * per_core + block_id % n_here
        in_halo = halo_id // n_halo * per_core + n_here + halo_id % n_halo
        return jnp.where(block_id < blocks_own, in_own, in_halo)

    ones = jnp.ones((16, 2 * tile), bf16)
    span = 1

    def attend_block(j, carry):
        b = s * n_here + j
        ids = [stored(tk_ref[b, t]) for t in range(slots)]
        q_rows = qbuf[block(j)]
        for pair in range(pairs):
            at = slice(pair * pw, (pair + 1) * pw)
            q_pair = q_rows[:, at]
            zero = jnp.zeros_like(q_pair)
            wide = jnp.concatenate(
                [jnp.where(low_half, q_pair, zero), jnp.where(low_half, zero, q_pair)], axis=0
            )
            top = jnp.full((8, 2 * tile), NEG_FILL, f32)
            for t in range(0, slots, span):
                lot = slice(t * tile, (t + span) * tile)
                keys = jnp.concatenate([kv[ids[t + u], pair] for u in range(span)], axis=0)
                bias = bias_ref[j, lot]
                scores = lax.dot_general(keys, wide, NT, preferred_element_type=f32)
                scores = scores + jnp.concatenate([bias, bias], axis=1)
                s_ref[pair, lot] = scores
                top = jnp.maximum(
                    top, jnp.max(scores.reshape(span * tile // 8, 8, 2 * tile), axis=0)
                )
            top = jnp.max(top, axis=0, keepdims=True)
            mixed = jnp.zeros((pw + 16, 2 * tile), f32)
            for t in range(0, slots, 2):
                p = jnp.exp2(s_ref[pair, t * tile : (t + 2) * tile] - top).astype(bf16)
                values = jnp.concatenate(
                    [kv[ids[t], pairs + pair], kv[ids[t + 1], pairs + pair]], axis=1
                )
                values = jnp.concatenate([values, ones], axis=0)
                mixed = mixed + jnp.dot(values, p, preferred_element_type=f32)
            inverse = 1.0 / mixed[pw : pw + 1]
            pieces = [
                mixed[:HD, :tile] * inverse[:, :tile],
                mixed[HD:pw, tile:] * inverse[:, tile:],
            ]
            att[c * pairs + pair, block(j)] = jnp.concatenate(pieces, axis=0).T.astype(bf16)
        t_copy(j).start()
        return carry

    with jax.named_scope("attend"):
        lax.fori_loop(0, n_here, attend_block, 0)

    loaded(6)

    def p_copy(j, to):
        src = half_part.at[j, far + to]
        dev = {"chan": 1 - c, "sub": to}
        return rdma(src, from_x.at[j, s], p_send, p_recv.at[j], dev)

    def p_wait(j):
        part = from_x.at[j]
        rdma(part, part, p_send, p_recv.at[j], xdev).wait_recv()

    def d_copy(j):
        return rdma(full_part.at[j, sib], from_sib.at[j], d_send, d_recv.at[j], sdev)

    def ffn_block(j, carry):
        with jax.named_scope("tw"):
            t_wait(j)
        at = block(j)
        mixed = jnp.concatenate([att[g, at] for g in range(2 * pairs)], axis=1)
        after = full_rows(at) + jnp.dot(mixed, wo[...], preferred_element_type=f32)
        normed_two = norm(after, 1).astype(bf16)
        hidden = gelu_tanh(
            lax.dot_general(normed_two, fin[...], NT, preferred_element_type=f32)
        ).astype(bf16)
        part = jnp.dot(hidden, fout[...], preferred_element_type=f32)
        for g in range(groups):
            half_part[j, g] = part[:, g * cols : (g + 1) * cols].astype(bf16)
        p_copy(j, 0).start()
        p_copy(j, 1).start()
        whole = part + after
        for g in range(groups):
            full_part[j, g] = whole[:, g * cols : (g + 1) * cols]
        d_copy(j).start()
        return carry

    with jax.named_scope("ffn"):
        lax.fori_loop(0, n_here, ffn_block, 0)

    in_block = lax.broadcasted_iota(jnp.int32, (tile, cols), 0)

    def finish(j, carry):
        with jax.named_scope("pw"):
            d_copy(j).wait_recv()
            p_wait(j)
        for core, kept in ((s, full_part[j, own]), (1 - s, from_sib[j])):
            base = core * half + j * tile
            summed = kept + from_x[j, core].astype(f32)
            done = jnp.where(base + in_block < live, summed, 0.0).astype(bf16)
            out_ref[pl.ds(pl.multiple_of(base, tile), tile)] = done
        return carry

    with jax.named_scope("finish"):
        lax.fori_loop(0, n_here, finish, 0)

    def sent(part, sem):
        rdma(part, part, sem, sem, sdev).wait_send()

    with jax.named_scope("endw"):
        sent(xq, x_send)
        sent(xq.at[own_half], a_send)
        sent(kv.at[pl.ds(s * per_core, per_core)], k_send.at[0])
        sent(att.at[pl.ds(c * pairs, pairs)], t_send)
        sent(half_part.at[:, pl.ds(far, 2)], p_send)
        sent(from_sib, d_send)

        @pl.when(has_up)
        def _():
            z_copy(1).wait_send()

        @pl.when(has_down)
        def _():
            z_copy(0).wait_send()

        @pl.when(has_halo)
        def _():
            sent(gx.at[pl.ds(c * 2, 2), halo_at], h_send)


def one_kernel(*args):
    (x, gains, shifts, wq, wk, wv, wo, fin, fout, live, send, tk, bits) = args
    f32, bf16 = jnp.float32, jnp.bfloat16
    rows, cols = x.shape
    width = gains.shape[1]
    groups = lax.axis_size("chan") * lax.axis_size("sub")
    halo = send.shape[-1]
    tile = bits.shape[-1]
    slots = tk.shape[1]
    ext = rows + 2 * halo
    head_cols = wq.shape[1]
    half = rows // 2
    pairs = head_cols // (2 * HD)
    n_here = half // tile
    n_halo = halo // tile
    vmem = pltpu.VMEM
    dma = pltpu.SemaphoreType.DMA
    in_any = pl.BlockSpec(memory_space=pl.ANY)
    return pl.pallas_call(
        layer_kernel,
        out_shape=pltpu.VMEM(x.shape, bf16),
        in_specs=[in_any] * 13,
        out_specs=pl.BlockSpec(memory_space=pltpu.VMEM),
        scratch_shapes=[
            vmem(x.shape, bf16),
            vmem((groups, half + halo, cols), bf16),
            vmem((2, halo, cols), bf16),
            vmem((ext // tile, 2 * pairs, tile, 2 * HD), bf16),
            vmem((head_cols, width), bf16),
            vmem((half, head_cols), bf16),
            vmem((n_here, slots * tile, tile), f32),
            vmem((pairs, slots * tile, 2 * tile), f32),
            vmem((2 * pairs, half, 2 * HD), bf16),
            vmem((n_here, groups, tile, cols), f32),
            vmem((n_here, groups, tile, cols), bf16),
            vmem((n_here, tile, cols), f32),
            vmem((n_here, 2, tile, cols), bf16),
            vmem((width, 3 * head_cols), bf16),
            vmem((2 * fin.shape[0] + wo.shape[0], width), bf16),
            vmem((2 * gains.shape[0], width), f32),
            vmem(send.shape, jnp.int32),
            vmem(bits.shape, jnp.int32),
            pltpu.SMEM(live.shape, jnp.int32),
            pltpu.SMEM(tk.shape, jnp.int32),
            dma((7,)),
            dma((2,)),
            dma,
            dma,
            dma,
            dma((n_here,)),
            dma((2,)),
            dma,
            dma,
            dma((n_halo,)),
            dma((1,)),
            dma((n_here + n_halo,)),
            dma,
            dma((n_here,)),
            dma,
            dma((n_here,)),
            dma,
            dma((n_here,)),
        ],
        compiler_params=pltpu.CompilerParams(collective_id=0, has_side_effects=True),
    )(*args)


def on_any_device(*args):
    two_by_two = lax.axis_size("chan") == 2 and lax.axis_size("sub") == 2
    cols, head_cols = args[0].shape[1], args[3].shape[1]
    tile, halo = args[12].shape[-1], args[10].shape[-1]
    rows_fit = args[0].shape[0] % (4 * tile) == 0 and halo % (2 * tile) == 0
    if two_by_two and cols % 128 == 0 and head_cols % (2 * HD) == 0 and rows_fit and args[11].shape[1] % 2 == 0:
        return one_kernel(*args)
    return on_device(*args)


def solution(mesh):
    in_specs = (
        P(("ens", "space"), ("chan", "sub")),
        P(),
        P(),
        P(None, "chan"),
        P(None, "chan"),
        P(None, "chan"),
        P(),
        P("chan", None),
        P("chan", None),
        P("space"),
        P("space", None, None),
        P("space", None),
        P("space", None, None, None),
    )
    out_specs = P(("ens", "space"), ("chan", "sub"))
    return jax.shard_map(
        on_any_device, mesh=mesh, in_specs=in_specs, out_specs=out_specs, check_vma=False
    )
```

time: 35.5 us -> 31 us (0.87)
  the two profiles are of different devices: /device:TPU:0 before, /device:TPU:13 now
where the time goes in v1:
time: 31 us; the launch traced here: 30.9 us
  Pallas kernels  29.5 us (95%)
  local copies, waits for them, and re-layouts  0.71 us (2%)
  between operations  0.66 us (2%)
    pallas_call x1, Pallas kernels, one_kernel(): pl.pallas_call(layer_kernel, out_shape=pltpu.VMEM(x.shape, bf16), in_spec...  29.5 us
    unnamed x1, local copies, waits for them, and re-layouts  0.71 us

profile of v1, /device:TPU:13, one launch (start us, length us, event | category | flops | bytes accessed | tf_op | source)
XLA Modules:
  0.0 30.9 jit_solution(6238613184113873832)
XLA Ops:
  0.7 29.5 %shard_map.127 = bf16[1024,128]{1,0:T(8,128)(2,1)S(1)} custom-call(bf16[1024,128]{1,0:T(8,128)(2,1)} %x_hbm.1, f32[2,512]{1,0:T(2,128)} %gains_hbm.1, f32[2,512]{1,0:T(2,128)} %shifts_hbm.1, bf16[512,256]{1,0:T(8,128)(2,1)} %wq_hbm.1, bf16[512,256]{1,0:T(8,128)(2,1)} %wk_hbm.1, bf16[512,256]{1,0:T(8,128)(2,1)} %wv_hbm.1, bf16[512,512]{1,0:T(8,128)(2,1)} %wo_hbm.1, ...), custom_call_target="tpu_custom_call" | custom-call | tf_op jit(solution)/shard_map/pallas_call | solution.py:673
  30.2 0.7 %copy.15 = bf16[1024,128]{1,0:T(8,128)(2,1)} copy(bf16[1024,128]{1,0:T(8,128)(2,1)S(1)} %shard_map.127) | data formatting | bytes 524288

commit v2 on v1

--- a/solution.py
+++ b/solution.py
@@ -218,6 +218,8 @@
     qbuf,
     bias_ref,
     s_ref,
+    o_ref,
+    l_ref,
     att,
     full_part,
     half_part,
@@ -264,6 +266,7 @@
     half = rows // 2
     n_here = half // tile
     n_halo = halo // tile
+    n_keys = blocks_own + 2 * n_halo
 
     c = lax.axis_index("chan")
     s = lax.axis_index("sub")
@@ -412,33 +415,47 @@
 
     live = live_ref[0]
     word_rows = tile // words
-    row_id = lax.broadcasted_iota(jnp.int32, (tile, tile), 0)
-    col_id = lax.broadcasted_iota(jnp.int32, (tile, tile), 1)
-    shifts = lax.broadcasted_iota(jnp.int32, (word_rows, tile), 0)
     low_half = lax.broadcasted_iota(jnp.int32, (tile, pw), 1) < HD
+    sub_row = lax.broadcasted_iota(jnp.int32, (8, tile), 0)
+    phase = sub_row % 4
+    high_nibble = sub_row // 4 * 4
+    lane = lax.broadcasted_iota(jnp.int32, (words, tile), 1)
+    first_key = lax.broadcasted_iota(jnp.int32, (words, tile), 0) * word_rows
+    own_bit = jnp.where(
+        lane // word_rows * word_rows == first_key,
+        jnp.left_shift(jnp.ones_like(lane), lane % word_rows),
+        0,
+    )
 
     def mask_block(j, carry):
         b = s * n_here + j
+        ids = [tk_ref[b, t] for t in range(slots)]
+        spread = []
         for t in range(slots):
-            slot_id = tk_ref[b, t]
-            block_bits = bits_ref[b, t]
-            set_bits = jnp.concatenate(
+            limit = jnp.where(ids[t] >= blocks_own, tile, live - ids[t] * tile)
+            count = jnp.clip(limit - first_key, 0, word_rows)
+            some = jnp.left_shift(jnp.ones_like(count), jnp.minimum(count, word_rows - 1)) - 1
+            good = jnp.where(count >= word_rows, -1, some)
+            if t == 0:
+                good = good | own_bit
+            kept = bits_ref[b, t] & good
+            spread.append(
                 [
-                    jnp.right_shift(
-                        jnp.broadcast_to(block_bits[w : w + 1, :], (word_rows, tile)), shifts
-                    )
-                    & 1
+                    jnp.right_shift(jnp.broadcast_to(kept[w : w + 1, :], (8, tile)), phase)
+                    & 0x11111111
                     for w in range(words)
-                ],
-                axis=0,
+                ]
             )
-            limit = jnp.where(slot_id >= blocks_own, tile, live - slot_id * tile)
-            good = row_id < limit
-            if t == 0:
-                good = good | (row_id == col_id)
-            bias_ref[j, t * tile : (t + 1) * tile] = jnp.where(
-                (set_bits == 1) & good, 0.0, NEG_FILL
-            )
+        for e in range(n_keys):
+            picks = [jnp.where(ids[t] == e, -1, 0) for t in range(slots)]
+            for w in range(words):
+                total = spread[0][w] & picks[0]
+                for t in range(1, slots):
+                    total = total + (spread[t][w] & picks[t])
+                for m in range(word_rows // 8):
+                    times = jnp.right_shift(total, high_nibble + 8 * m) & 15
+                    at = e * tile + w * word_rows + m * 8
+                    bias_ref[j, at : at + 8] = jnp.maximum(jnp.log2(times.astype(f32)), NEG_FILL)
         return carry
 
     with jax.named_scope("mask"):
@@ -500,7 +517,88 @@
                 h_copy(k).start()
 
     lax.fori_loop(early, n_here, own_step, 0)
-    for k in range(n_halo):
+    def t_copy(j):
+        part = att.at[pl.ds(c * pairs, pairs), block(j)]
+        return rdma(part, part, t_send, t_recv.at[j], xdev)
+
+    def t_wait(j):
+        part = att.at[pl.ds((1 - c) * pairs, pairs), block(j)]
+        rdma(part, part, t_send, t_recv.at[j], xdev).wait_recv()
+
+    def stored(e):
+        if e < blocks_own:
+            return e // n_here * per_core + e % n_here
+        e -= blocks_own
+        return e // n_halo * per_core + n_here + e % n_halo
+
+    ones = jnp.ones((16, 2 * tile), bf16)
+
+    def scores_of(j, pair, keys_at):
+        q_pair = qbuf[block(j), pair * pw : (pair + 1) * pw]
+        zero = jnp.zeros_like(q_pair)
+        wide = jnp.concatenate(
+            [jnp.where(low_half, q_pair, zero), jnp.where(low_half, zero, q_pair)], axis=0
+        )
+        top = jnp.full((8, 2 * tile), NEG_FILL, f32)
+        for n, e in enumerate(keys_at):
+            bias = bias_ref[j, e * tile : (e + 1) * tile]
+            scores = lax.dot_general(kv[stored(e), pair], wide, NT, preferred_element_type=f32)
+            scores = scores + jnp.concatenate([bias, bias], axis=1)
+            s_ref[pair, n * tile : (n + 1) * tile] = scores
+            top = jnp.maximum(top, jnp.max(scores.reshape(tile // 8, 8, 2 * tile), axis=0))
+        return jnp.max(top, axis=0, keepdims=True)
+
+    def mixed_of(pair, keys_at, top):
+        mixed = jnp.zeros((pw + 16, 2 * tile), f32)
+        for n in range(0, len(keys_at), 2):
+            p = jnp.exp2(s_ref[pair, n * tile : (n + 2) * tile] - top).astype(bf16)
+            values = jnp.concatenate(
+                [kv[stored(keys_at[n]), pairs + pair], kv[stored(keys_at[n + 1]), pairs + pair]],
+                axis=1,
+            )
+            values = jnp.concatenate([values, ones], axis=0)
+            mixed = mixed + jnp.dot(values, p, preferred_element_type=f32)
+        heads = jnp.concatenate([mixed[:HD, :tile], mixed[HD:pw, tile:]], axis=0)
+        return heads, mixed[pw : pw + 8]
+
+    def both_heads(row):
+        return jnp.concatenate(
+            [
+                jnp.broadcast_to(row[:, :tile], (HD, tile)),
+                jnp.broadcast_to(row[:, tile:], (HD, tile)),
+            ],
+            axis=0,
+        )
+
+    own_keys = tuple(range(blocks_own))
+    halo_keys = tuple(range(blocks_own, n_keys))
+
+    def attend_own(j):
+        tops = [scores_of(j, pair, own_keys) for pair in range(pairs)]
+        for pair in range(pairs):
+            heads, sums = mixed_of(pair, own_keys, tops[pair])
+            o_ref[j, pair] = heads
+            l_ref[j, pair, :8] = sums
+            l_ref[j, pair, 8:] = jnp.broadcast_to(tops[pair], (8, 2 * tile))
+
+    def attend_halo(j):
+        tops = [scores_of(j, pair, halo_keys) for pair in range(pairs)]
+        for pair in range(pairs):
+            before = l_ref[j, pair, 8:9]
+            top = jnp.maximum(tops[pair], before)
+            shrink = jnp.exp2(before - top)
+            heads, sums = mixed_of(pair, halo_keys, top)
+            total = l_ref[j, pair, :1] * shrink + sums[:1]
+            heads = o_ref[j, pair] * both_heads(shrink) + heads
+            heads = heads * both_heads(1.0 / total)
+            att[c * pairs + pair, block(j)] = heads.T.astype(bf16)
+        t_copy(j).start()
+
+    with jax.named_scope("kvw"):
+        for i in range(n_here):
+            k_copy(1 - s, i).wait_recv()
+
+    def halo_step(k, carry):
         with jax.named_scope("hw"):
 
             @pl.when(has_halo)
@@ -509,70 +607,34 @@
 
         with jax.named_scope("hproj"):
             project(n_here + k, False)
-
-    with jax.named_scope("kvw"):
-        for i in range(n_here + n_halo):
+        return carry
+
+    def first_step(j, carry):
+        with jax.named_scope("aown"):
+            attend_own(j)
+        return carry
+
+    lax.fori_loop(0, 1, first_step, 0)
+    lax.fori_loop(0, n_halo, halo_step, 0)
+    lax.fori_loop(1, early, first_step, 0)
+    with jax.named_scope("kvw2"):
+        for i in range(n_here, n_here + n_halo):
             k_copy(1 - s, i).wait_recv()
 
-    def t_copy(j):
-        part = att.at[pl.ds(c * pairs, pairs), block(j)]
-        return rdma(part, part, t_send, t_recv.at[j], xdev)
-
-    def t_wait(j):
-        part = att.at[pl.ds((1 - c) * pairs, pairs), block(j)]
-        rdma(part, part, t_send, t_recv.at[j], xdev).wait_recv()
-
-    def stored(block_id):
-        halo_id = block_id - blocks_own
-        in_own = block_id // n_here * per_core + block_id % n_here
-        in_halo = halo_id // n_halo * per_core + n_here + halo_id % n_halo
-        return jnp.where(block_id < blocks_own, in_own, in_halo)
-
-    ones = jnp.ones((16, 2 * tile), bf16)
-    span = 1
-
-    def attend_block(j, carry):
-        b = s * n_here + j
-        ids = [stored(tk_ref[b, t]) for t in range(slots)]
-        q_rows = qbuf[block(j)]
-        for pair in range(pairs):
-            at = slice(pair * pw, (pair + 1) * pw)
-            q_pair = q_rows[:, at]
-            zero = jnp.zeros_like(q_pair)
-            wide = jnp.concatenate(
-                [jnp.where(low_half, q_pair, zero), jnp.where(low_half, zero, q_pair)], axis=0
-            )
-            top = jnp.full((8, 2 * tile), NEG_FILL, f32)
-            for t in range(0, slots, span):
-                lot = slice(t * tile, (t + span) * tile)
-                keys = jnp.concatenate([kv[ids[t + u], pair] for u in range(span)], axis=0)
-                bias = bias_ref[j, lot]
-                scores = lax.dot_general(keys, wide, NT, preferred_element_type=f32)
-                scores = scores + jnp.concatenate([bias, bias], axis=1)
-                s_ref[pair, lot] = scores
-                top = jnp.maximum(
-                    top, jnp.max(scores.reshape(span * tile // 8, 8, 2 * tile), axis=0)
-                )
-            top = jnp.max(top, axis=0, keepdims=True)
-            mixed = jnp.zeros((pw + 16, 2 * tile), f32)
-            for t in range(0, slots, 2):
-                p = jnp.exp2(s_ref[pair, t * tile : (t + 2) * tile] - top).astype(bf16)
-                values = jnp.concatenate(
-                    [kv[ids[t], pairs + pair], kv[ids[t + 1], pairs + pair]], axis=1
-                )
-                values = jnp.concatenate([values, ones], axis=0)
-                mixed = mixed + jnp.dot(values, p, preferred_element_type=f32)
-            inverse = 1.0 / mixed[pw : pw + 1]
-            pieces = [
-                mixed[:HD, :tile] * inverse[:, :tile],
-                mixed[HD:pw, tile:] * inverse[:, tile:],
-            ]
-            att[c * pairs + pair, block(j)] = jnp.concatenate(pieces, axis=0).T.astype(bf16)
-        t_copy(j).start()
+    def second_step(j, carry):
+        with jax.named_scope("ahalo"):
+            attend_halo(j)
+        with jax.named_scope("aown"):
+            attend_own(j + early)
         return carry
 
-    with jax.named_scope("attend"):
-        lax.fori_loop(0, n_here, attend_block, 0)
+    def third_step(j, carry):
+        with jax.named_scope("ahalo"):
+            attend_halo(j)
+        return carry
+
+    lax.fori_loop(0, n_here - early, second_step, 0)
+    lax.fori_loop(n_here - early, n_here, third_step, 0)
 
     loaded(6)
 
@@ -682,8 +744,10 @@
             vmem((ext // tile, 2 * pairs, tile, 2 * HD), bf16),
             vmem((head_cols, width), bf16),
             vmem((half, head_cols), bf16),
-            vmem((n_here, slots * tile, tile), f32),
-            vmem((pairs, slots * tile, 2 * tile), f32),
+            vmem((n_here, ext, tile), f32),
+            vmem((pairs, rows, 2 * tile), f32),
+            vmem((n_here, pairs, 2 * HD, tile), f32),
+            vmem((n_here, pairs, 16, 2 * tile), f32),
             vmem((2 * pairs, half, 2 * HD), bf16),
             vmem((n_here, groups, tile, cols), f32),
             vmem((n_here, groups, tile, cols), bf16),
@@ -724,7 +788,8 @@
     cols, head_cols = args[0].shape[1], args[3].shape[1]
     tile, halo = args[12].shape[-1], args[10].shape[-1]
     rows_fit = args[0].shape[0] % (4 * tile) == 0 and halo % (2 * tile) == 0
-    if two_by_two and cols % 128 == 0 and head_cols % (2 * HD) == 0 and rows_fit and args[11].shape[1] % 2 == 0:
+    few_slots = args[11].shape[1] < 16 and args[12].shape[-2] * 32 == tile and tile == cols
+    if two_by_two and cols % 128 == 0 and head_cols % (2 * HD) == 0 and rows_fit and few_slots:
         return one_kernel(*args)
     return on_device(*args)
 

time: 31 us -> 30.1 us (0.971)
  the two profiles are of different devices: /device:TPU:13 before, /device:TPU:0 now
where the time goes in v2:
time: 30.1 us; the launch traced here: 30 us
  Pallas kernels  28.6 us (95%)
  local copies, waits for them, and re-layouts  0.71 us (2%)
  between operations  0.66 us (2%)
    pallas_call x1, Pallas kernels, one_kernel(): pl.pallas_call(layer_kernel, out_shape=pltpu.VMEM(x.shape, bf16), in_spec...  28.6 us
    unnamed x1, local copies, waits for them, and re-layouts  0.71 us

profile of v2, /device:TPU:0, one launch (start us, length us, event | category | flops | bytes accessed | tf_op | source)
XLA Modules:
  0.0 30.0 jit_solution(13653272110328999904)
XLA Ops:
  0.7 28.6 %shard_map.127 = bf16[1024,128]{1,0:T(8,128)(2,1)S(1)} custom-call(bf16[1024,128]{1,0:T(8,128)(2,1)} %x_hbm.1, f32[2,512]{1,0:T(2,128)} %gains_hbm.1, f32[2,512]{1,0:T(2,128)} %shifts_hbm.1, bf16[512,256]{1,0:T(8,128)(2,1)} %wq_hbm.1, bf16[512,256]{1,0:T(8,128)(2,1)} %wk_hbm.1, bf16[512,256]{1,0:T(8,128)(2,1)} %wv_hbm.1, bf16[512,512]{1,0:T(8,128)(2,1)} %wo_hbm.1, ...), custom_call_target="tpu_custom_call" | custom-call | tf_op jit(solution)/shard_map/pallas_call | solution.py:735
  29.3 0.7 %copy.15 = bf16[1024,128]{1,0:T(8,128)(2,1)} copy(bf16[1024,128]{1,0:T(8,128)(2,1)S(1)} %shard_map.127) | data formatting | bytes 524288

commit v3 on v2

--- a/solution.py
+++ b/solution.py
@@ -247,7 +247,6 @@
     t_send,
     t_recv,
     p_send,
-    p_recv,
     d_send,
     d_recv,
 ):
@@ -280,6 +279,9 @@
     has_up = z < nz - 1
     has_down = z > 0
     has_halo = jnp.where(s == 0, z, nz - 1 - z) > 0
+    sib_halo = jnp.where(s == 0, nz - 1 - z, z) > 0
+    per_core = n_here + n_halo
+    last = n_here - 1
 
     own_half = pl.ds(pl.multiple_of(s * half, half), half)
     sib_half = pl.ds(pl.multiple_of((1 - s) * half, half), half)
@@ -334,6 +336,7 @@
         pltpu.make_async_copy(a, b, w_sem.at[i]).start()
     with jax.named_scope("barrierw"):
         pl.semaphore_wait(barrier, 3 + jnp.where(has_up, 2, 0) + jnp.where(has_down, 2, 0))
+    with jax.named_scope("localw"):
         local.wait()
 
     def rdma(src, dst, ss, rs, dev):
@@ -381,7 +384,7 @@
         part = gx.at[pl.ds(far, 2), pl.ds(half + k * tile, tile)]
         rdma(part, part, h_send, h_recv.at[k], xdev).wait_recv()
 
-    for i in range(n_here):
+    for i in range(last):
         x_copy(i, 0).start()
         x_copy(i, 1).start()
     a_copy().start()
@@ -405,9 +408,12 @@
     def _():
         z_copy(0).start()
 
-    @pl.when(jnp.logical_not(has_halo))
-    def _():
-        gx[:, halo_at, :] = jnp.zeros((groups, halo, cols), bf16)
+    for core, there in ((s, has_halo), (1 - s, sib_halo)):
+
+        @pl.when(jnp.logical_not(there))
+        def _():
+            empty = jnp.zeros((n_halo, 2 * pairs, tile, pw), bf16)
+            kv[pl.ds(core * per_core + n_here, n_halo)] = empty
 
     for i in range(1, 5):
         loaded(i)
@@ -473,13 +479,16 @@
 
     scale = LOG2E / math.sqrt(HD)
 
-    per_core = n_here + n_halo
-
-    def k_copy(core, i):
-        part = kv.at[core * per_core + i]
-        return rdma(part, part, k_send.at[0], k_recv.at[i], sdev)
-
-    def project(i, with_queries):
+    def k_copy(i, kind):
+        part = kv.at[s * per_core + i]
+        return rdma(part, part, k_send.at[kind % 2], k_recv.at[kind], sdev)
+
+    def k_wait(first, count, kind):
+        part = kv.at[pl.ds((1 - s) * per_core + first, count)]
+        rdma(part, part, k_send.at[0], k_recv.at[kind], sdev).wait_recv()
+
+    def project(i, kind):
+        with_queries = kind != 1
         normed = norm(full_rows(block(i)), 0).astype(bf16)
         to = s * per_core + i
         wanted = (2 if with_queries else 1) * head_cols
@@ -491,7 +500,7 @@
         values = lax.dot_general(wvt[...], normed, NT, preferred_element_type=f32)
         for pair in range(pairs):
             kv[to, pairs + pair] = values[pair * pw : (pair + 1) * pw].astype(bf16)
-        k_copy(s, i).start()
+        k_copy(i, kind).start()
 
     loaded(5)
     local_own.wait()
@@ -502,11 +511,10 @@
         with jax.named_scope("xw"):
             x_wait(i)
         with jax.named_scope("proj"):
-            project(i, True)
+            project(i, 0)
         return carry
 
-    early = n_here // 2
-    lax.fori_loop(0, early, own_step, 0)
+    lax.fori_loop(0, 1, own_step, 0)
 
     with jax.named_scope("zw"):
 
@@ -516,9 +524,28 @@
             for k in range(n_halo):
                 h_copy(k).start()
 
-    lax.fori_loop(early, n_here, own_step, 0)
-    def t_copy(j):
-        part = att.at[pl.ds(c * pairs, pairs), block(j)]
+    x_copy(last, 0).start()
+    x_copy(last, 1).start()
+    lax.fori_loop(1, last, own_step, 0)
+
+    @pl.when(has_halo)
+    def _():
+        def halo_step(k, carry):
+            with jax.named_scope("hw"):
+                h_wait(k)
+            with jax.named_scope("hproj"):
+                project(n_here + k, 1)
+            return carry
+
+        lax.fori_loop(0, n_halo, halo_step, 0)
+
+    with jax.named_scope("xw"):
+        x_wait(last)
+    with jax.named_scope("proj"):
+        project(last, 2)
+
+    def t_copy(j, first, count):
+        part = att.at[pl.ds(c * pairs + first, count), block(j)]
         return rdma(part, part, t_send, t_recv.at[j], xdev)
 
     def t_wait(j):
@@ -570,82 +597,65 @@
             axis=0,
         )
 
-    own_keys = tuple(range(blocks_own))
-    halo_keys = tuple(range(blocks_own, n_keys))
-
-    def attend_own(j):
-        tops = [scores_of(j, pair, own_keys) for pair in range(pairs)]
+    late_keys = tuple(e for e in range(blocks_own) if e % n_here == last)
+    early_keys = tuple(e for e in range(n_keys) if e not in late_keys)
+    all_keys = early_keys + late_keys
+
+    def attend_early(j):
+        tops = [scores_of(j, pair, early_keys) for pair in range(pairs)]
         for pair in range(pairs):
-            heads, sums = mixed_of(pair, own_keys, tops[pair])
-            o_ref[j, pair] = heads
-            l_ref[j, pair, :8] = sums
-            l_ref[j, pair, 8:] = jnp.broadcast_to(tops[pair], (8, 2 * tile))
-
-    def attend_halo(j):
-        tops = [scores_of(j, pair, halo_keys) for pair in range(pairs)]
-        for pair in range(pairs):
-            before = l_ref[j, pair, 8:9]
-            top = jnp.maximum(tops[pair], before)
-            shrink = jnp.exp2(before - top)
-            heads, sums = mixed_of(pair, halo_keys, top)
-            total = l_ref[j, pair, :1] * shrink + sums[:1]
-            heads = o_ref[j, pair] * both_heads(shrink) + heads
-            heads = heads * both_heads(1.0 / total)
-            att[c * pairs + pair, block(j)] = heads.T.astype(bf16)
-        t_copy(j).start()
+            heads, sums = mixed_of(pair, early_keys, tops[pair])
+            o_ref[pair] = heads
+            l_ref[pair, :8] = sums
+            l_ref[pair, 8:] = jnp.broadcast_to(tops[pair], (8, 2 * tile))
+
+    def attend_late(j, pair):
+        before = l_ref[pair, 8:9]
+        top = jnp.maximum(scores_of(j, pair, late_keys), before)
+        shrink = jnp.exp2(before - top)
+        heads, sums = mixed_of(pair, late_keys, top)
+        total = l_ref[pair, :1] * shrink + sums[:1]
+        heads = o_ref[pair] * both_heads(shrink) + heads
+        heads = heads * both_heads(1.0 / total)
+        att[c * pairs + pair, block(j)] = heads.T.astype(bf16)
+        t_copy(j, pair, 1).start()
+
+    def attend_all(j, carry):
+        with jax.named_scope("aall"):
+            tops = [scores_of(j, pair, all_keys) for pair in range(pairs)]
+            for pair in range(pairs):
+                heads, sums = mixed_of(pair, all_keys, tops[pair])
+                heads = heads * both_heads(1.0 / sums[:1])
+                att[c * pairs + pair, block(j)] = heads.T.astype(bf16)
+            t_copy(j, 0, pairs).start()
+        return carry
 
     with jax.named_scope("kvw"):
-        for i in range(n_here):
-            k_copy(1 - s, i).wait_recv()
-
-    def halo_step(k, carry):
-        with jax.named_scope("hw"):
-
-            @pl.when(has_halo)
-            def _():
-                h_wait(k)
-
-        with jax.named_scope("hproj"):
-            project(n_here + k, False)
-        return carry
-
-    def first_step(j, carry):
-        with jax.named_scope("aown"):
-            attend_own(j)
-        return carry
-
-    lax.fori_loop(0, 1, first_step, 0)
-    lax.fori_loop(0, n_halo, halo_step, 0)
-    lax.fori_loop(1, early, first_step, 0)
+        k_wait(0, last, 0)
+
+        @pl.when(sib_halo)
+        def _():
+            k_wait(n_here, n_halo, 1)
+
+    with jax.named_scope("early"):
+        attend_early(0)
     with jax.named_scope("kvw2"):
-        for i in range(n_here, n_here + n_halo):
-            k_copy(1 - s, i).wait_recv()
-
-    def second_step(j, carry):
-        with jax.named_scope("ahalo"):
-            attend_halo(j)
-        with jax.named_scope("aown"):
-            attend_own(j + early)
-        return carry
-
-    def third_step(j, carry):
-        with jax.named_scope("ahalo"):
-            attend_halo(j)
-        return carry
-
-    lax.fori_loop(0, n_here - early, second_step, 0)
-    lax.fori_loop(n_here - early, n_here, third_step, 0)
+        k_wait(last, 1, 2)
+    for pair in range(pairs):
+        with jax.named_scope("late"):
+            attend_late(0, pair)
+    lax.fori_loop(1, n_here, attend_all, 0)
 
     loaded(6)
 
     def p_copy(j, to):
         src = half_part.at[j, far + to]
         dev = {"chan": 1 - c, "sub": to}
-        return rdma(src, from_x.at[j, s], p_send, p_recv.at[j], dev)
+        return rdma(src, from_x.at[j, s], p_send, x_recv.at[j], dev)
 
     def p_wait(j):
         part = from_x.at[j]
-        rdma(part, part, p_send, p_recv.at[j], xdev).wait_recv()
+        rdma(part, part, p_send, x_recv.at[j], xdev).wait_recv()
 
     def d_copy(j):
         return rdma(full_part.at[j, sib], from_sib.at[j], d_send, d_recv.at[j], sdev)
@@ -696,7 +706,7 @@
     with jax.named_scope("endw"):
         sent(xq, x_send)
         sent(xq.at[own_half], a_send)
-        sent(kv.at[pl.ds(s * per_core, per_core)], k_send.at[0])
+        sent(kv.at[pl.ds(s * per_core, n_here)], k_send.at[0])
         sent(att.at[pl.ds(c * pairs, pairs)], t_send)
         sent(half_part.at[:, pl.ds(far, 2)], p_send)
         sent(from_sib, d_send)
@@ -712,6 +722,7 @@
         @pl.when(has_halo)
         def _():
             sent(gx.at[pl.ds(c * 2, 2), halo_at], h_send)
+            sent(kv.at[pl.ds(s * per_core + n_here, n_halo)], k_send.at[1])
 
 
 def one_kernel(*args):
@@ -745,9 +756,9 @@
             vmem((head_cols, width), bf16),
             vmem((half, head_cols), bf16),
             vmem((n_here, ext, tile), f32),
-            vmem((pairs, rows, 2 * tile), f32),
-            vmem((n_here, pairs, 2 * HD, tile), f32),
-            vmem((n_here, pairs, 16, 2 * tile), f32),
+            vmem((pairs, ext, 2 * tile), f32),
+            vmem((pairs, 2 * HD, tile), f32),
+            vmem((pairs, 16, 2 * tile), f32),
             vmem((2 * pairs, half, 2 * HD), bf16),
             vmem((n_here, groups, tile, cols), f32),
             vmem((n_here, groups, tile, cols), bf16),
@@ -770,12 +781,11 @@
             dma,
             dma,
             dma((n_halo,)),
-            dma((1,)),
-            dma((n_here + n_halo,)),
+            dma((2,)),
+            dma((3,)),
             dma,
             dma((n_here,)),
             dma,
-            dma((n_here,)),
             dma,
             dma((n_here,)),
         ],

time: 30.1 us -> 29.6 us (0.983); the launches traced: 30 us -> 29.1 us
  Pallas kernels: 28.6 us -> 27.7 us
    pallas_call x1, Pallas kernels: 28.6 us -> 27.7 us  [one_kernel(): pl.pallas_call(layer_kernel, out_shape=pltpu.VMEM(x.shape, bf16), in_spec...]
where the time goes in v3:
time: 29.6 us; the launch traced here: 29.1 us
  Pallas kernels  27.7 us (94%)
  local copies, waits for them, and re-layouts  0.71 us (2%)
  between operations  0.66 us (2%)
    pallas_call x1, Pallas kernels, one_kernel(): pl.pallas_call(layer_kernel, out_shape=pltpu.VMEM(x.shape, bf16), in_spec...  27.7 us
    unnamed x1, local copies, waits for them, and re-layouts  0.71 us

profile of v3, /device:TPU:0, one launch (start us, length us, event | category | flops | bytes accessed | tf_op | source)
XLA Modules:
  0.0 29.1 jit_solution(6798912495997374910)
XLA Ops:
  0.7 27.7 %shard_map.127 = bf16[1024,128]{1,0:T(8,128)(2,1)S(1)} custom-call(bf16[1024,128]{1,0:T(8,128)(2,1)} %x_hbm.1, f32[2,512]{1,0:T(2,128)} %gains_hbm.1, f32[2,512]{1,0:T(2,128)} %shifts_hbm.1, bf16[512,256]{1,0:T(8,128)(2,1)} %wq_hbm.1, bf16[512,256]{1,0:T(8,128)(2,1)} %wk_hbm.1, bf16[512,256]{1,0:T(8,128)(2,1)} %wv_hbm.1, bf16[512,512]{1,0:T(8,128)(2,1)} %wo_hbm.1, ...), custom_call_target="tpu_custom_call" | custom-call | tf_op jit(solution)/shard_map/pallas_call | solution.py:746
  28.4 0.7 %copy.15 = bf16[1024,128]{1,0:T(8,128)(2,1)} copy(bf16[1024,128]{1,0:T(8,128)(2,1)S(1)} %shard_map.127) | data formatting | bytes 524288

commit v4 on v3

--- a/solution.py
+++ b/solution.py
@@ -248,7 +248,6 @@
     t_recv,
     p_send,
     d_send,
-    d_recv,
 ):
     f32, bf16 = jnp.float32, jnp.bfloat16
     rows, cols = x_hbm.shape
@@ -320,22 +319,18 @@
     greet({"chan": 1 - c, "sub": 1 - s})
     greet(sdev)
 
-    @pl.when(has_up)
+    @pl.when(has_halo)
     def _():
-        greet({"space": z + 1})
-        greet({"space": z + 1, "sub": 1 - s})
-
-    @pl.when(has_down)
-    def _():
-        greet({"space": z - 1})
-        greet({"space": z - 1, "sub": 1 - s})
+        feeder = z - 1 + 2 * s
+        greet({"space": feeder})
+        greet({"space": feeder, "sub": 1 - s})
 
     local.start()
     local_own.start()
     for a, b, i in loads:
         pltpu.make_async_copy(a, b, w_sem.at[i]).start()
     with jax.named_scope("barrierw"):
-        pl.semaphore_wait(barrier, 3 + jnp.where(has_up, 2, 0) + jnp.where(has_down, 2, 0))
+        pl.semaphore_wait(barrier, 3 + jnp.where(has_up, 1, 0) + jnp.where(has_down, 1, 0))
     with jax.named_scope("localw"):
         local.wait()
 
@@ -479,28 +474,42 @@
 
     scale = LOG2E / math.sqrt(HD)
 
-    def k_copy(i, kind):
-        part = kv.at[s * per_core + i]
+    def kv_copy(i, first, count, kind):
+        part = kv.at[s * per_core + i, pl.ds(first, count)]
         return rdma(part, part, k_send.at[kind % 2], k_recv.at[kind], sdev)
 
     def k_wait(first, count, kind):
         part = kv.at[pl.ds((1 - s) * per_core + first, count)]
         rdma(part, part, k_send.at[0], k_recv.at[kind], sdev).wait_recv()
 
+    def half_wait(i, first, kind):
+        part = kv.at[(1 - s) * per_core + i, pl.ds(first, pairs)]
+        rdma(part, part, k_send.at[0], k_recv.at[kind], sdev).wait_recv()
+
     def project(i, kind):
-        with_queries = kind != 1
         normed = norm(full_rows(block(i)), 0).astype(bf16)
         to = s * per_core + i
-        wanted = (2 if with_queries else 1) * head_cols
+        wanted = (2 if kind == 0 else 1) * head_cols
         both = jnp.dot(normed, proj_w[:, :wanted], preferred_element_type=f32)
         for pair in range(pairs):
             kv[to, pair] = both[:, pair * pw : (pair + 1) * pw].astype(bf16)
-        if with_queries:
-            qbuf[block(i)] = (both[:, head_cols:] * scale).astype(bf16)
+        if kind == 2:
+            kv_copy(i, 0, pairs, 2).start()
         values = lax.dot_general(wvt[...], normed, NT, preferred_element_type=f32)
         for pair in range(pairs):
             kv[to, pairs + pair] = values[pair * pw : (pair + 1) * pw].astype(bf16)
-        k_copy(i, kind).start()
+        if kind == 2:
+            kv_copy(i, pairs, pairs, 4).start()
+        else:
+            kv_copy(i, 0, 2 * pairs, kind).start()
+        if kind == 0:
+            queries = both[:, head_cols:]
+        elif kind == 2:
+            queries = jnp.dot(
+                normed, proj_w[:, head_cols : 2 * head_cols], preferred_element_type=f32
+            )
+        if kind != 1:
+            qbuf[block(i)] = (queries * scale).astype(bf16)
 
     loaded(5)
     local_own.wait()
@@ -527,22 +536,6 @@
     x_copy(last, 0).start()
     x_copy(last, 1).start()
     lax.fori_loop(1, last, own_step, 0)
-
-    @pl.when(has_halo)
-    def _():
-        def halo_step(k, carry):
-            with jax.named_scope("hw"):
-                h_wait(k)
-            with jax.named_scope("hproj"):
-                project(n_here + k, 1)
-            return carry
-
-        lax.fori_loop(0, n_halo, halo_step, 0)
-
-    with jax.named_scope("xw"):
-        x_wait(last)
-    with jax.named_scope("proj"):
-        project(last, 2)
 
     def t_copy(j, first, count):
         part = att.at[pl.ds(c * pairs + first, count), block(j)]
@@ -598,55 +591,100 @@
         )
 
     late_keys = tuple(e for e in range(blocks_own) if e % n_here == last)
-    early_keys = tuple(e for e in range(n_keys) if e not in late_keys)
-    all_keys = early_keys + late_keys
-
-    def attend_early(j):
-        tops = [scores_of(j, pair, early_keys) for pair in range(pairs)]
+    early_keys = tuple(e for e in range(blocks_own) if e not in late_keys)
+    halo_keys = tuple(range(blocks_own, n_keys))
+    all_keys = early_keys + halo_keys + late_keys
+
+    def attend_some(j, keys_at, first):
+        tops = [scores_of(j, pair, keys_at) for pair in range(pairs)]
         for pair in range(pairs):
-            heads, sums = mixed_of(pair, early_keys, tops[pair])
+            top = tops[pair]
+            if not first:
+                before = l_ref[pair, 8:9]
+                top = jnp.maximum(top, before)
+                shrink = jnp.exp2(before - top)
+            heads, sums = mixed_of(pair, keys_at, top)
+            if not first:
+                heads = o_ref[pair] * both_heads(shrink) + heads
+                sums = l_ref[pair, :8] * shrink + sums
             o_ref[pair] = heads
             l_ref[pair, :8] = sums
-            l_ref[pair, 8:] = jnp.broadcast_to(tops[pair], (8, 2 * tile))
+            l_ref[pair, 8:] = jnp.broadcast_to(top, (8, 2 * tile))
 
     def attend_late(j, pair):
         before = l_ref[pair, 8:9]
         top = jnp.maximum(scores_of(j, pair, late_keys), before)
         shrink = jnp.exp2(before - top)
+        if pair == 0:
+            half_wait(last, pairs, 4)
         heads, sums = mixed_of(pair, late_keys, top)
         total = l_ref[pair, :1] * shrink + sums[:1]
         heads = o_ref[pair] * both_heads(shrink) + heads
         heads = heads * both_heads(1.0 / total)
         att[c * pairs + pair, block(j)] = heads.T.astype(bf16)
-        t_copy(j, pair, 1).start()
-
-    def attend_all(j, carry):
+
+    def finish_pair(j, pair, top):
+        heads, sums = mixed_of(pair, all_keys, top)
+        heads = heads * both_heads(1.0 / sums[:1])
+        att[c * pairs + pair, block(j)] = heads.T.astype(bf16)
+
+    def attend_all(j, top):
         with jax.named_scope("aall"):
-            tops = [scores_of(j, pair, all_keys) for pair in range(pairs)]
             for pair in range(pairs):
-                heads, sums = mixed_of(pair, all_keys, tops[pair])
-                heads = heads * both_heads(1.0 / sums[:1])
-                att[c * pairs + pair, block(j)] = heads.T.astype(bf16)
-            t_copy(j, 0, pairs).start()
-        return carry
-
+                finish_pair(j, pair, top)
+                following = j if pair + 1 < pairs else j + 1
+                top = scores_of(following, (pair + 1) % pairs, all_keys)
+                t_copy(j, pair, 1).start()
+        return top
+
+    def attend_end(j, top):
+        for pair in range(pairs):
+            finish_pair(j, pair, top)
+            if pair + 1 < pairs:
+                top = scores_of(j, pair + 1, all_keys)
+            t_copy(j, pair, 1).start()
+
+    def halo_step(k):
+        @pl.when(has_halo)
+        def _():
+            with jax.named_scope("hw"):
+                h_wait(k)
+            with jax.named_scope("hproj"):
+                project(n_here + k, 1)
+
+    halo_step(0)
     with jax.named_scope("kvw"):
         k_wait(0, last, 0)
+    with jax.named_scope("early"):
+        attend_some(0, early_keys, True)
+    for k in range(1, n_halo):
+        halo_step(k)
+    with jax.named_scope("xw"):
+        x_wait(last)
+    with jax.named_scope("proj"):
+        project(last, 2)
+    with jax.named_scope("kvw1"):
 
         @pl.when(sib_halo)
         def _():
             k_wait(n_here, n_halo, 1)
 
-    with jax.named_scope("early"):
-        attend_early(0)
+    with jax.named_scope("ehalo"):
+        attend_some(0, halo_keys, False)
     with jax.named_scope("kvw2"):
-        k_wait(last, 1, 2)
+        half_wait(last, 0, 2)
     for pair in range(pairs):
         with jax.named_scope("late"):
             attend_late(0, pair)
-    lax.fori_loop(1, n_here, attend_all, 0)
+            if pair + 1 == pairs:
+                top = scores_of(1, 0, all_keys)
+            t_copy(0, pair, 1).start()
+    top = lax.fori_loop(1, last, attend_all, top)
+    with jax.named_scope("aend"):
+        attend_end(last, top)
 
     loaded(6)
+    landed_part = full_part.at[:, pl.ds(0, 2)]
 
     def p_copy(j, to):
         src = half_part.at[j, far + to]
@@ -654,11 +692,11 @@
         return rdma(src, from_x.at[j, s], p_send, x_recv.at[j], dev)
 
     def p_wait(j):
-        part = from_x.at[j]
+        part = landed_part.at[j]
         rdma(part, part, p_send, x_recv.at[j], xdev).wait_recv()
 
     def d_copy(j):
-        return rdma(full_part.at[j, sib], from_sib.at[j], d_send, d_recv.at[j], sdev)
+        return rdma(full_part.at[j, sib], from_sib.at[j], d_send, x_recv.at[j], sdev)
 
     def ffn_block(j, carry):
         with jax.named_scope("tw"):
@@ -688,7 +726,6 @@
 
     def finish(j, carry):
         with jax.named_scope("pw"):
-            d_copy(j).wait_recv()
             p_wait(j)
         for core, kept in ((s, full_part[j, own]), (1 - s, from_sib[j])):
             base = core * half + j * tile
@@ -782,12 +819,11 @@
             dma,
             dma((n_halo,)),
             dma((2,)),
-            dma((3,)),
+            dma((5,)),
             dma,
             dma((n_here,)),
             dma,
             dma,
-            dma((n_here,)),
         ],
         compiler_params=pltpu.CompilerParams(collective_id=0, has_side_effects=True),
     )(*args)

time: 29.6 us -> 29.1 us (0.983)
  Pallas kernels: 27.7 us -> 27.4 us
where the time goes in v4:
time: 29.1 us; the launch traced here: 28.8 us
  Pallas kernels  27.4 us (94%)
  local copies, waits for them, and re-layouts  0.71 us (2%)
  between operations  0.66 us (2%)
    pallas_call x1, Pallas kernels, one_kernel(): pl.pallas_call(layer_kernel, out_shape=pltpu.VMEM(x.shape, bf16), in_spec...  27.4 us
    unnamed x1, local copies, waits for them, and re-layouts  0.71 us

profile of v4, /device:TPU:0, one launch (start us, length us, event | category | flops | bytes accessed | tf_op | source)
XLA Modules:
  0.0 28.8 jit_solution(13922876808068401070)
XLA Ops:
  0.7 27.4 %shard_map.127 = bf16[1024,128]{1,0:T(8,128)(2,1)S(1)} custom-call(bf16[1024,128]{1,0:T(8,128)(2,1)} %x_hbm.1, f32[2,512]{1,0:T(2,128)} %gains_hbm.1, f32[2,512]{1,0:T(2,128)} %shifts_hbm.1, bf16[512,256]{1,0:T(8,128)(2,1)} %wq_hbm.1, bf16[512,256]{1,0:T(8,128)(2,1)} %wk_hbm.1, bf16[512,256]{1,0:T(8,128)(2,1)} %wv_hbm.1, bf16[512,512]{1,0:T(8,128)(2,1)} %wo_hbm.1, ...), custom_call_target="tpu_custom_call" | custom-call | tf_op jit(solution)/shard_map/pallas_call | solution.py:783
  28.1 0.7 %copy.15 = bf16[1024,128]{1,0:T(8,128)(2,1)} copy(bf16[1024,128]{1,0:T(8,128)(2,1)S(1)} %shard_map.127) | data formatting | bytes 524288
